TPU v7x, 256 devices: a whole 4x4x8 slice. The times are simulated.
256 devices in a mesh: group: 2 (over y_hi), gx: 8 (over z), gy: 16 (over x, y_lo, core).
Axes of the slice: x: 4, y: 4 (y_hi: 2, y_lo: 2; y = y_hi * 2 + y_lo), z: 8, core: 2. Of those that a mesh axis runs over, the one named last changes fastest.
Arguments:
- displacement: float32 [2, 3, 64, 256, 128], P('group', None, 'gx', 'gy'), may hold values from -6 to 6
- velocity: float32 [2, 3, 64, 256, 128], P('group', None, 'gx', 'gy'), may hold values from -6 to 6
- modulus: float32 [2, 64, 256, 128], P('group', 'gx', 'gy'), may hold values from 1 to 4
- bond_words: int32 [2, 64, 256, 128], P(None, 'gx', 'gy'), may hold values from 0 to 2147483647, as said below
- coupling_map: int32 [3, 64, 256], P(None, 'gx', 'gy'), may hold values from 0 to 2
Outputs:
- new_displacement: float32 [2, 3, 64, 256, 128], P('group', None, 'gx', 'gy')
- new_velocity: float32 [2, 3, 64, 256, 128], P('group', None, 'gx', 'gy')
Inputs may be any that keep to these rules, and one draw needn't show every extreme that they name: `bond_words`: bonds to positions outside the zone are 0; bit 30 of word 1 is 0.
All inputs are finite; a program needn't handle non-finite values.
Results may differ from a plain program's by a relative error of at most 0.0001.
Values sent between devices are 32-bit elements; how exact they have to be, the bound alone decides.
A program may use at most 64 MiB of HBM per device.

v0:
```python
import math

import jax
import jax.numpy as jnp
import numpy as np
from jax import lax
from jax.sharding import PartitionSpec as P

time_step = 0.1
bond_scale = 1.0


def with_halo(block, sides, width):
    for axis, dim in sides:
        count = lax.axis_size(axis)
        forward = [(i, i + 1) for i in range(count - 1)]
        backward = [(target, source) for source, target in forward]
        low = lax.ppermute(
            lax.slice_in_dim(block, block.shape[dim] - width, None, axis=dim), axis, forward
        )
        high = lax.ppermute(lax.slice_in_dim(block, 0, width, axis=dim), axis, backward)
        block = jnp.concatenate([low, block, high], axis=dim)
    return block


def passed_along(block, axis, distance):
    devices = range(lax.axis_size(axis))
    route = [(i - distance, i) for i in devices if i - distance in devices]
    return lax.ppermute(block, axis, route)


def half_offsets():
    table = []
    for delta_x in range(-3, 4):
        for delta_y in range(-3, 4):
            for delta_z in range(-3, 4):
                radius = delta_x * delta_x + delta_y * delta_y + delta_z * delta_z
                if 0 < radius <= 9 and (delta_x, delta_y, delta_z) > (0, 0, 0):
                    table.append((delta_x, delta_y, delta_z))
    return table


def hex_stiffness():
    poisson = 0.3
    lame_first = poisson / ((1.0 + poisson) * (1.0 - 2.0 * poisson))
    shear_modulus = 0.5 / (1.0 + poisson)
    elastic = np.zeros((6, 6))
    elastic[:3, :3] = lame_first
    for axis_id in range(3):
        elastic[axis_id, axis_id] += 2.0 * shear_modulus
        elastic[3 + axis_id, 3 + axis_id] = shear_modulus
    points = [0.5 - 0.5 / math.sqrt(3.0), 0.5 + 0.5 / math.sqrt(3.0)]
    result = np.zeros((24, 24))
    shear_pairs = ((0, 1), (1, 2), (0, 2))
    for along_x in points:
        for along_y in points:
            for along_z in points:
                coords = (along_x, along_y, along_z)
                gradients = np.zeros((3, 8))
                for corner in range(8):
                    corner_bits = (corner >> 2 & 1, corner >> 1 & 1, corner & 1)
                    factors = [
                        coords[axis_id] if corner_bits[axis_id] else 1.0 - coords[axis_id]
                        for axis_id in range(3)
                    ]
                    slopes = [1.0 if corner_bits[axis_id] else -1.0 for axis_id in range(3)]
                    gradients[0, corner] = slopes[0] * factors[1] * factors[2]
                    gradients[1, corner] = factors[0] * slopes[1] * factors[2]
                    gradients[2, corner] = factors[0] * factors[1] * slopes[2]
                strain = np.zeros((6, 24))
                for axis_id in range(3):
                    strain[axis_id, axis_id * 8 : axis_id * 8 + 8] = gradients[axis_id]
                for shear_row, pair in enumerate(shear_pairs):
                    left_axis, right_axis = pair
                    strain[3 + shear_row, left_axis * 8 : left_axis * 8 + 8] = gradients[right_axis]
                    strain[3 + shear_row, right_axis * 8 : right_axis * 8 + 8] = gradients[
                        left_axis
                    ]
                result += strain.T @ elastic @ strain / 8.0
    return result


def bond_sum(field_pad, words_pad, modulus_pad, size_x, size_y, size_z):

    def window(array, delta_x, delta_y, delta_z):
        return array[
            ...,
            3 + delta_x : 3 + delta_x + size_x,
            3 + delta_y : 3 + delta_y + size_y,
            3 + delta_z : 3 + delta_z + size_z,
        ]

    centre = window(field_pad, 0, 0, 0)
    centre_modulus = window(modulus_pad, 0, 0, 0)
    centre_words = window(words_pad, 0, 0, 0)
    summed = jnp.zeros_like(centre)
    for number, offset in enumerate(half_offsets()):
        delta_x, delta_y, delta_z = offset
        word_id = number // 31
        bit_id = number % 31
        factor = (
            0.5
            * bond_scale
            / float(delta_x * delta_x + delta_y * delta_y + delta_z * delta_z) ** 1.5
        )
        ahead_diff = window(field_pad, delta_x, delta_y, delta_z) - centre
        behind_diff = window(field_pad, -delta_x, -delta_y, -delta_z) - centre
        ahead_proj = delta_x * ahead_diff[0] + delta_y * ahead_diff[1] + delta_z * ahead_diff[2]
        behind_proj = delta_x * behind_diff[0] + delta_y * behind_diff[1] + delta_z * behind_diff[2]
        ahead_flag = (centre_words[word_id] >> bit_id & 1).astype(jnp.float32)
        behind_flag = (
            window(words_pad[word_id], -delta_x, -delta_y, -delta_z) >> bit_id & 1
        ).astype(jnp.float32)
        strength = (
            ahead_flag
            * (centre_modulus + window(modulus_pad, delta_x, delta_y, delta_z))
            * ahead_proj
        )
        strength = (
            strength
            + behind_flag
            * (centre_modulus + window(modulus_pad, -delta_x, -delta_y, -delta_z))
            * behind_proj
        )
        strength = factor * strength
        summed = summed + jnp.stack([delta_x * strength, delta_y * strength, delta_z * strength])
    return summed


def couple(below_top, map_layers):
    coupled = jnp.zeros_like(below_top)
    for layer_id in range(below_top.shape[3]):
        coupled = coupled + jnp.where(
            map_layers[None] == layer_id, below_top[..., layer_id : layer_id + 1], 0.0
        )
    return coupled


def spread(reaction, map_layers):
    columns = []
    for layer_id in range(reaction.shape[3]):
        columns.append(jnp.sum(jnp.where(map_layers[None] == layer_id, reaction, 0.0), axis=3))
    return jnp.stack(columns, axis=3)


def slab_forces(extended, modulus_rim, start_x, start_y, full_x, full_y, rows_x, rows_y, depth_z):
    stiffness = jnp.asarray(hex_stiffness(), dtype=jnp.float32)
    field_pad = jnp.pad(extended, ((0, 0), (0, 0), (0, 0), (0, 1)))
    pieces = []
    for component in range(3):
        for corner in range(8):
            corner_x, corner_y, corner_z = (corner >> 2 & 1, corner >> 1 & 1, corner & 1)
            pieces.append(
                field_pad[
                    component,
                    2 + corner_x : 3 + corner_x + rows_x,
                    2 + corner_y : 3 + corner_y + rows_y,
                    corner_z : corner_z + depth_z,
                ]
            )
    gathered = jnp.stack(pieces).reshape(24, -1)
    global_x = start_x - 1 + jnp.arange(rows_x + 1)
    global_y = start_y - 1 + jnp.arange(rows_y + 1)
    inside = (
        ((global_x >= 0) & (global_x < full_x - 1))[:, None, None]
        & ((global_y >= 0) & (global_y < full_y - 1))[None, :, None]
        & (jnp.arange(depth_z) < depth_z - 1)[None, None, :]
    ).astype(jnp.float32)
    element_modulus = modulus_rim[2 : 3 + rows_x, 2 : 3 + rows_y, :] * inside
    result = jnp.dot(
        stiffness, gathered, precision=lax.Precision.HIGHEST, preferred_element_type=jnp.float32
    )
    result = result.reshape(24, rows_x + 1, rows_y + 1, depth_z) * element_modulus[None]
    result_pad = jnp.pad(result, ((0, 0), (0, 0), (0, 0), (1, 0)))
    forces = []
    for component in range(3):
        summed = jnp.zeros((rows_x, rows_y, depth_z), jnp.float32)
        for corner in range(8):
            corner_x, corner_y, corner_z = (corner >> 2 & 1, corner >> 1 & 1, corner & 1)
            summed = (
                summed
                - result_pad[
                    component * 8 + corner,
                    1 - corner_x : 1 - corner_x + rows_x,
                    1 - corner_y : 1 - corner_y + rows_y,
                    1 - corner_z : 1 - corner_z + depth_z,
                ]
            )
        forces.append(summed)
    return jnp.stack(forces)


def per_device(displacement, velocity, modulus, bond_words, coupling_map):
    rows_x, rows_y, depth_z = (displacement.shape[2], displacement.shape[3], displacement.shape[4])
    layers = coupling_map.shape[0]
    full_x = rows_x * lax.axis_size("gx")
    full_y = rows_y * lax.axis_size("gy")
    start_x = lax.axis_index("gx") * rows_x
    start_y = lax.axis_index("gy") * rows_y
    is_zone = lax.axis_index("group") == 0
    words_rim = with_halo(bond_words, (("gx", 1), ("gy", 2)), 3)
    modulus_rim = with_halo(modulus[0], (("gx", 0), ("gy", 1)), 3)
    map_layers = jnp.transpose(coupling_map, (1, 2, 0))
    z_padding = ((0, 0), (0, 0), (0, 0), (3, 3))
    words_pad = jnp.pad(words_rim, z_padding)
    modulus_pad = jnp.pad(modulus_rim, ((0, 0), (0, 0), (3, 3)))
    layer_ids = jnp.arange(depth_z)
    moving = (layer_ids >= layers)[None, None, None, :]
    unclamped = (layer_ids > 0)[None, None, None, :]
    position_x = start_x + jnp.arange(rows_x)
    position_y = start_y + jnp.arange(rows_y)
    count_x = (position_x > 0).astype(jnp.float32) + (position_x < full_x - 1).astype(jnp.float32)
    count_y = (position_y > 0).astype(jnp.float32) + (position_y < full_y - 1).astype(jnp.float32)
    count_z = (layer_ids > 0).astype(jnp.float32) + (layer_ids < depth_z - 1).astype(jnp.float32)
    lumped_mass = count_x[:, None, None] * count_y[None, :, None] * count_z[None, None, :] / 8.0
    current = displacement[0]
    velocity_now = velocity[0]
    below_top = passed_along(current[:, :, :, depth_z - layers :], "group", -1)
    coupled = couple(below_top, map_layers)
    current = jnp.where(
        is_zone, jnp.concatenate([coupled, current[:, :, :, layers:]], axis=3), current
    )
    extended = with_halo(current, (("gx", 1), ("gy", 2)), 3)

    def zone_branch():
        return bond_sum(
            jnp.pad(extended, z_padding), words_pad, modulus_pad, rows_x, rows_y, depth_z
        )

    def slab_branch():
        return slab_forces(
            extended, modulus_rim, start_x, start_y, full_x, full_y, rows_x, rows_y, depth_z
        )

    forces = lax.cond(is_zone, zone_branch, slab_branch)
    reaction = passed_along(forces[:, :, :, :layers], "group", 1)
    interface = jnp.pad(
        spread(reaction, map_layers), ((0, 0), (0, 0), (0, 0), (depth_z - layers, 0))
    )
    slab_total = forces + interface
    zone_velocity = jnp.where(moving, velocity_now + time_step * forces, velocity_now)
    zone_field = jnp.where(moving, current + time_step * zone_velocity, current)
    slab_velocity = jnp.where(unclamped, velocity_now + time_step * slab_total / lumped_mass, 0.0)
    slab_field = jnp.where(unclamped, current + time_step * slab_velocity, 0.0)
    velocity_now = jnp.where(is_zone, zone_velocity, slab_velocity)
    current = jnp.where(is_zone, zone_field, slab_field)
    return (current[None], velocity_now[None])


def solution(mesh):
    return jax.shard_map(
        per_device,
        mesh=mesh,
        in_specs=(
            P("group", None, "gx", "gy", None),
            P("group", None, "gx", "gy", None),
            P("group", "gx", "gy", None),
            P(None, "gx", "gy", None),
            P(None, "gx", "gy"),
        ),
        out_specs=(P("group", None, "gx", "gy", None), P("group", None, "gx", "gy", None)),
        check_vma=False,
    )
```

profile of v0, /device:TPU:118, one launch (start us, length us, event | category | flops | bytes accessed | tf_op | source)
XLA Modules:
  0.0 117.7 jit_solution(7653052499667735561)
XLA Ops:
  2.2 2.2 %collective-permute-start = (f32[3,8,16,3]{2,1,0,3:T(8,128)S(1)}, f32[3,8,16,3]{2,1,0,3:T(8,128)S(1)}, u32[]{:S(2)}, u32[]{:S(2)}) collective-permute-start(f32[3,8,16,3]{2,1,0,3:T(8,128)S(1)} %slice.2951), channel_id=1, source_target_pairs={{128,0},{129,1},{130,2},{131,3},{132,4},{133,5},{134,6},{135,7},{1... | collective-permute-start | bytes 13832 | tf_op jit(solution)/shard_map/ppermute | solution.py:29
  5.2 2.0 %collective-permute-start.6 = (f32[3,16,128]{2,1,0:T(8,128)S(1)}, f32[3,16,128]{2,1,0:T(8,128)S(1)}, u32[]{:S(2)}, u32[]{:S(2)}) collective-permute-start(f32[3,16,128]{2,1,0:T(8,128)S(1)} %get-tuple-element.425), channel_id=1, source_target_pairs={{16,0},{32,16},{48,32},{64,48},{80,64},{96,80},{112,96},{17,1},{33... | collective-permute-start | bytes 73736 | tf_op jit(solution)/shard_map/ppermute | solution.py:21
  7.2 5.0 %collective-permute-start.5 = (f32[3,16,128]{2,1,0:T(8,128)S(1)}, f32[3,16,128]{2,1,0:T(8,128)S(1)}, u32[]{:S(2)}, u32[]{:S(2)}) collective-permute-start(f32[3,16,128]{2,1,0:T(8,128)S(1)} %get-tuple-element.424), channel_id=1, source_target_pairs={{0,16},{16,32},{32,48},{48,64},{64,80},{80,96},{96,112},{1,17},{17... | collective-permute-start | bytes 73736 | tf_op jit(solution)/shard_map/ppermute | solution.py:18
  13.7 3.8 %collective-permute-start.9 = (s32[2,3,16,128]{3,2,1,0:T(8,128)S(1)}, s32[2,3,16,128]{3,2,1,0:T(8,128)}, u32[]{:S(2)}, u32[]{:S(2)}) collective-permute-start(s32[2,3,16,128]{3,2,1,0:T(8,128)S(1)} %get-tuple-element.421), channel_id=1, source_target_pairs={{0,16},{16,32},{32,48},{48,64},{64,80},{80,96},{96,112},{1,17},{17... | collective-permute-start | bytes 147464 | tf_op jit(solution)/shard_map/ppermute | solution.py:18
  17.5 2.0 %collective-permute-start.10 = (s32[2,3,16,128]{3,2,1,0:T(8,128)}, s32[2,3,16,128]{3,2,1,0:T(8,128)}, u32[]{:S(2)}, u32[]{:S(2)}) collective-permute-start(s32[2,3,16,128]{3,2,1,0:T(8,128)} %get-tuple-element.420), channel_id=1, source_target_pairs={{16,0},{32,16},{48,32},{64,48},{80,64},{96,80},{112,96},{17,1},{33... | collective-permute-start | bytes 147464 | tf_op jit(solution)/shard_map/ppermute | solution.py:21
  25.1 2.6 %collective-permute-start.8 = (f32[14,3,128]{2,1,0:T(4,128)S(1)}, f32[14,3,128]{2,1,0:T(4,128)S(1)}, u32[]{:S(2)}, u32[]{:S(2)}) collective-permute-start(f32[14,3,128]{2,1,0:T(4,128)S(1)} %get-tuple-element.423), channel_id=1, source_target_pairs={{1,0},{2,1},{3,2},{4,3},{5,4},{6,5},{7,6},{8,7},{9,8},{10,9},{11,1... | collective-permute-start | bytes 64520 | tf_op jit(solution)/shard_map/ppermute | solution.py:21
  27.7 2.1 %collective-permute-start.7 = (f32[14,3,128]{2,1,0:T(4,128)S(1)}, f32[14,3,128]{2,1,0:T(4,128)S(1)}, u32[]{:S(2)}, u32[]{:S(2)}) collective-permute-start(f32[14,3,128]{2,1,0:T(4,128)S(1)} %get-tuple-element.422), channel_id=1, source_target_pairs={{0,1},{1,2},{2,3},{3,4},{4,5},{5,6},{6,7},{7,8},{8,9},{9,10},{10,1... | collective-permute-start | bytes 64520 | tf_op jit(solution)/shard_map/ppermute | solution.py:18
  29.8 2.2 %fusion.1075 = (f32[3,3,16,128]{2,1,0,3:T(4,128)S(1)}, f32[3,3,16,128]{2,1,0,3:T(4,128)S(1)}) fusion(f32[3,8,16,128]{2,1,0,3:T(8,128)} %maximum_select_fusion), kind=kLoop, calls=%fused_computation.1850 | loop fusion | bytes 294912 | tf_op jit(solution)/shard_map/slice | solution.py:19
  32.2 2.2 %collective-permute-start.2 = (f32[3,3,16,128]{3,2,1,0:T(8,128)S(1)}, f32[3,3,16,128]{3,2,1,0:T(8,128)S(1)}, u32[]{:S(2)}, u32[]{:S(2)}) collective-permute-start(f32[3,3,16,128]{3,2,1,0:T(8,128)S(1)} %copy.45), channel_id=1, source_target_pairs={{16,0},{32,16},{48,32},{64,48},{80,64},{96,80},{112,96},{17,1},{33... | collective-permute-start | bytes 221192 | tf_op jit(solution)/shard_map/ppermute | solution.py:21
  34.7 4.9 %collective-permute-start.1 = (f32[3,3,16,128]{3,2,1,0:T(8,128)S(1)}, f32[3,3,16,128]{3,2,1,0:T(8,128)S(1)}, u32[]{:S(2)}, u32[]{:S(2)}) collective-permute-start(f32[3,3,16,128]{3,2,1,0:T(8,128)S(1)} %copy.44), channel_id=1, source_target_pairs={{0,16},{16,32},{32,48},{48,64},{64,80},{80,96},{96,112},{1,17},{17... | collective-permute-start | bytes 221192 | tf_op jit(solution)/shard_map/ppermute | solution.py:18
  42.0 4.0 %collective-permute-start.12 = (s32[2,14,3,128]{3,2,1,0:T(4,128)}, s32[2,14,3,128]{3,2,1,0:T(4,128)}, u32[]{:S(2)}, u32[]{:S(2)}) collective-permute-start(s32[2,14,3,128]{3,2,1,0:T(4,128)} %get-tuple-element.419), channel_id=1, source_target_pairs={{1,0},{2,1},{3,2},{4,3},{5,4},{6,5},{7,6},{8,7},{9,8},{10,9},{11,1... | collective-permute-start | bytes 129032 | tf_op jit(solution)/shard_map/ppermute | solution.py:21
  45.9 1.9 %collective-permute-start.11 = (s32[2,14,3,128]{3,2,1,0:T(4,128)}, s32[2,14,3,128]{3,2,1,0:T(4,128)}, u32[]{:S(2)}, u32[]{:S(2)}) collective-permute-start(s32[2,14,3,128]{3,2,1,0:T(4,128)} %get-tuple-element.418), channel_id=1, source_target_pairs={{0,1},{1,2},{2,3},{3,4},{4,5},{5,6},{6,7},{7,8},{8,9},{9,10},{10,1... | collective-permute-start | bytes 129032 | tf_op jit(solution)/shard_map/ppermute | solution.py:18
  50.2 2.6 %pad_maximum_fusion.1 = f32[3,14,16,128]{2,1,0,3:T(8,128)S(1)} fusion(f32[3,3,16,128]{2,1,0,3:T(4,128)} %copy.47, f32[3,8,16,128]{2,1,0,3:T(8,128)} %maximum_select_fusion, f32[3,3,16,128]{2,1,0,3:T(4,128)} %copy.46), kind=kLoop, calls=%fused_computation.1800 | loop fusion | flops 172032 | bytes 688128 | tf_op jit(solution)/shard_map/concatenate | solution.py:22
  52.7 3.6 %fusion.1074 = (f32[3,14,3,128]{2,1,0,3:T(8,128)}, f32[3,14,3,128]{2,1,0,3:T(8,128)}) fusion(f32[3,14,16,128]{2,1,0,3:T(8,128)S(1)} %pad_maximum_fusion.1), kind=kLoop, calls=%fused_computation.1849 | loop fusion | bytes 258048 | tf_op jit(solution)/shard_map/slice | solution.py:19
  58.1 3.1 %copy.49 = f32[3,14,3,128]{3,1,2,0:T(8,128)} copy(f32[3,14,3,128]{2,1,0,3:T(8,128)} %get-tuple-element.415) | data formatting | bytes 129024 | tf_op jit(solution)/shard_map/slice | solution.py:21
  61.3 4.5 %collective-permute-start.4 = (f32[3,14,3,128]{3,1,2,0:T(8,128)}, f32[3,14,3,128]{3,1,2,0:T(8,128)}, u32[]{:S(2)}, u32[]{:S(2)}) collective-permute-start(f32[3,14,3,128]{3,1,2,0:T(8,128)} %copy.49), channel_id=1, source_target_pairs={{1,0},{2,1},{3,2},{4,3},{5,4},{6,5},{7,6},{8,7},{9,8},{10,9},{11,1... | collective-permute-start | bytes 193544 | tf_op jit(solution)/shard_map/ppermute | solution.py:21
  67.6 1.9 %collective-permute-start.3 = (f32[3,14,3,128]{3,1,2,0:T(8,128)}, f32[3,14,3,128]{3,1,2,0:T(8,128)S(1)}, u32[]{:S(2)}, u32[]{:S(2)}) collective-permute-start(f32[3,14,3,128]{3,1,2,0:T(8,128)} %copy.48), channel_id=1, source_target_pairs={{0,1},{1,2},{2,3},{3,4},{4,5},{5,6},{6,7},{7,8},{8,9},{9,10},{10,1... | collective-permute-start | bytes 193544 | tf_op jit(solution)/shard_map/ppermute | solution.py:18
  71.4 3.0 %collective-permute-done.3 = f32[3,14,3,128]{3,1,2,0:T(8,128)S(1)} collective-permute-done((f32[3,14,3,128]{3,1,2,0:T(8,128)}, f32[3,14,3,128]{3,1,2,0:T(8,128)S(1)}, u32[]{:S(2)}, u32[]{:S(2)}) %collective-permute-start.3) | collective-permute-done | bytes 64544 | tf_op jit(solution)/shard_map/ppermute | solution.py:18
  75.5 24.0 %conditional.1 = (f32[3,8,16,128]{3,2,1,0:T(8,128)S(1)}) conditional(s32[]{:T(128)} %convert_element_type.605, (f32[3,14,22,128]{3,2,1,0:T(8,128)S(1)}, s32[]{:T(128)}, s32[]{:T(128)}, f32[14,22,128]{2,1,0:T(8,128)S(1)}) %tuple.18, (s32[2,14,22,128]{3,2,1,0:T(8,128)S(1)}, f32[14,22,128]{2,1,0:T(8,128)S(1)}, ...), branch_computations={%region_0.1_spmd.clone, %region_1.2_spmd} | conditional | flops 136365696 | bytes 112835016 | solution.py:235
  92.2 1.8 %reshape.1197 = f32[24,19584]{1,0:T(8,128)S(1)} reshape(f32[24,9,17,128]{3,2,1,0:T(8,128)} %fusion.982) | data formatting | bytes 3760128 | tf_op jit(solution)/shard_map/cond/branch_0_fun/reshape | solution.py:161
  94.1 2.9 %fusion.1078 = f32[24,19584]{1,0:T(8,128)} fusion(f32[24,24]{1,0:T(8,128)S(1)} %copy-done.8, f32[24,19584]{1,0:T(8,128)S(1)} %reshape.1197), kind=kOutput, calls=%fused_computation.1853 | convolution fusion | flops 135364608 | bytes 3762432 | tf_op jit(solution)/shard_map/cond/branch_0_fun/dot_general | solution.py:170
  103.7 4.7 %collective-permute-done.13 = f32[3,8,16,3]{2,1,0,3:T(8,128)} collective-permute-done((f32[3,8,16,3]{2,1,0,3:T(8,128)}, f32[3,8,16,3]{2,1,0,3:T(8,128)}, u32[]{:S(2)}, u32[]{:S(2)}) %collective-permute-start.13) | collective-permute-done | bytes 4640 | tf_op jit(solution)/shard_map/ppermute | solution.py:29
  109.2 4.7 %select_bitcast_fusion = (f32[1,3,8,16,128]{3,2,1,4,0:T(8,128)}, f32[1,3,8,16,128]{3,2,1,4,0:T(8,128)}) fusion(pred[]{:T(512)S(6)} %eq.27, f32[3,8,16,128]{2,1,0,3:T(8,128)} %copy.54, f32[1,3,8,16,128]{3,2,1,4,0:T(8,128)S(1)} %copy-done.1, pred[128]{0:T(512)(128)(4,1)} %get-tuple-element.433, f32[8,16,128]{1,0,2:T(8,128)} %multiply_multiply_fusion, ...), kind=kLoop, calls=%fused_computation.1814 | loop fusion | flops 1032192 | bytes 1250049 | tf_op jit(solution)/shard_map/broadcast_in_dim | solution.py:247
  113.9 2.6 %copy.57 = f32[1,3,8,16,128]{4,3,2,1,0:T(8,128)} copy(f32[1,3,8,16,128]{3,2,1,4,0:T(8,128)} %get-tuple-element.413) | data formatting | bytes 393216
  (104 shorter events, 45.9 us)
Async XLA Ops:
  0.6 21.4 %copy-start.5 = (f32[1,3,8,16,128]{4,3,2,1,0:T(8,128)S(1)}, f32[1,3,8,16,128]{4,3,2,1,0:T(8,128)}, u32[]{:S(2)}) copy-start(f32[1,3,8,16,128]{4,3,2,1,0:T(8,128)} %param.9) | copy-start | bytes 589828
  2.2 21.5 %collective-permute-start = (f32[3,8,16,3]{2,1,0,3:T(8,128)S(1)}, f32[3,8,16,3]{2,1,0,3:T(8,128)S(1)}, u32[]{:S(2)}, u32[]{:S(2)}) collective-permute-start(f32[3,8,16,3]{2,1,0,3:T(8,128)S(1)} %slice.2951), channel_id=1, source_target_pairs={{128,0},{129,1},{130,2},{131,3},{132,4},{133,5},{134,6},{135,7},{1... | collective-permute-start | bytes 13832 | tf_op jit(solution)/shard_map/ppermute | solution.py:29
  5.2 19.9 %collective-permute-start.6 = (f32[3,16,128]{2,1,0:T(8,128)S(1)}, f32[3,16,128]{2,1,0:T(8,128)S(1)}, u32[]{:S(2)}, u32[]{:S(2)}) collective-permute-start(f32[3,16,128]{2,1,0:T(8,128)S(1)} %get-tuple-element.425), channel_id=1, source_target_pairs={{16,0},{32,16},{48,32},{64,48},{80,64},{96,80},{112,96},{17,1},{33... | collective-permute-start | bytes 73736 | tf_op jit(solution)/shard_map/ppermute | solution.py:21
  7.2 17.9 %collective-permute-start.5 = (f32[3,16,128]{2,1,0:T(8,128)S(1)}, f32[3,16,128]{2,1,0:T(8,128)S(1)}, u32[]{:S(2)}, u32[]{:S(2)}) collective-permute-start(f32[3,16,128]{2,1,0:T(8,128)S(1)} %get-tuple-element.424), channel_id=1, source_target_pairs={{0,16},{16,32},{32,48},{48,64},{64,80},{80,96},{96,112},{1,17},{17... | collective-permute-start | bytes 73736 | tf_op jit(solution)/shard_map/ppermute | solution.py:18
  13.7 26.0 %collective-permute-start.9 = (s32[2,3,16,128]{3,2,1,0:T(8,128)S(1)}, s32[2,3,16,128]{3,2,1,0:T(8,128)}, u32[]{:S(2)}, u32[]{:S(2)}) collective-permute-start(s32[2,3,16,128]{3,2,1,0:T(8,128)S(1)} %get-tuple-element.421), channel_id=1, source_target_pairs={{0,16},{16,32},{32,48},{48,64},{64,80},{80,96},{96,112},{1,17},{17... | collective-permute-start | bytes 147464 | tf_op jit(solution)/shard_map/ppermute | solution.py:18
  17.5 23.0 %collective-permute-start.10 = (s32[2,3,16,128]{3,2,1,0:T(8,128)}, s32[2,3,16,128]{3,2,1,0:T(8,128)}, u32[]{:S(2)}, u32[]{:S(2)}) collective-permute-start(s32[2,3,16,128]{3,2,1,0:T(8,128)} %get-tuple-element.420), channel_id=1, source_target_pairs={{16,0},{32,16},{48,32},{64,48},{80,64},{96,80},{112,96},{17,1},{33... | collective-permute-start | bytes 147464 | tf_op jit(solution)/shard_map/ppermute | solution.py:21
  20.3 3.4 %copy-start.6 = (pred[8,16,3]{1,0,2:T(8,128)(4,1)}, pred[8,16,3]{1,0,2:T(8,128)(4,1)S(1)}, u32[]{:S(2)}) copy-start(pred[8,16,3]{1,0,2:T(8,128)(4,1)S(1)} %get-tuple-element.431) | copy-start | bytes 1156
  23.7 1.4 %copy-start.3 = (f32[1,8,16,128]{3,2,1,0:T(8,128)S(1)}, f32[1,8,16,128]{3,2,1,0:T(8,128)}, u32[]{:S(2)}) copy-start(f32[1,8,16,128]{3,2,1,0:T(8,128)} %param.10) | copy-start | bytes 196612
  25.1 9.6 %collective-permute-start.8 = (f32[14,3,128]{2,1,0:T(4,128)S(1)}, f32[14,3,128]{2,1,0:T(4,128)S(1)}, u32[]{:S(2)}, u32[]{:S(2)}) collective-permute-start(f32[14,3,128]{2,1,0:T(4,128)S(1)} %get-tuple-element.423), channel_id=1, source_target_pairs={{1,0},{2,1},{3,2},{4,3},{5,4},{6,5},{7,6},{8,7},{9,8},{10,9},{11,1... | collective-permute-start | bytes 64520 | tf_op jit(solution)/shard_map/ppermute | solution.py:21
  27.7 12.8 %copy-start.4 = (s32[2,8,16,128]{3,2,1,0:T(8,128)S(1)}, s32[2,8,16,128]{3,2,1,0:T(8,128)}, u32[]{:S(2)}) copy-start(s32[2,8,16,128]{3,2,1,0:T(8,128)} %param.11) | copy-start | bytes 393220
  27.7 11.9 %collective-permute-start.7 = (f32[14,3,128]{2,1,0:T(4,128)S(1)}, f32[14,3,128]{2,1,0:T(4,128)S(1)}, u32[]{:S(2)}, u32[]{:S(2)}) collective-permute-start(f32[14,3,128]{2,1,0:T(4,128)S(1)} %get-tuple-element.422), channel_id=1, source_target_pairs={{0,1},{1,2},{2,3},{3,4},{4,5},{5,6},{6,7},{7,8},{8,9},{9,10},{10,1... | collective-permute-start | bytes 64520 | tf_op jit(solution)/shard_map/ppermute | solution.py:18
  32.2 15.6 %collective-permute-start.2 = (f32[3,3,16,128]{3,2,1,0:T(8,128)S(1)}, f32[3,3,16,128]{3,2,1,0:T(8,128)S(1)}, u32[]{:S(2)}, u32[]{:S(2)}) collective-permute-start(f32[3,3,16,128]{3,2,1,0:T(8,128)S(1)} %copy.45), channel_id=1, source_target_pairs={{16,0},{32,16},{48,32},{64,48},{80,64},{96,80},{112,96},{17,1},{33... | collective-permute-start | bytes 221192 | tf_op jit(solution)/shard_map/ppermute | solution.py:21
  34.7 14.3 %collective-permute-start.1 = (f32[3,3,16,128]{3,2,1,0:T(8,128)S(1)}, f32[3,3,16,128]{3,2,1,0:T(8,128)S(1)}, u32[]{:S(2)}, u32[]{:S(2)}) collective-permute-start(f32[3,3,16,128]{3,2,1,0:T(8,128)S(1)} %copy.44), channel_id=1, source_target_pairs={{0,16},{16,32},{32,48},{48,64},{64,80},{80,96},{96,112},{1,17},{17... | collective-permute-start | bytes 221192 | tf_op jit(solution)/shard_map/ppermute | solution.py:18
  42.0 27.6 %collective-permute-start.12 = (s32[2,14,3,128]{3,2,1,0:T(4,128)}, s32[2,14,3,128]{3,2,1,0:T(4,128)}, u32[]{:S(2)}, u32[]{:S(2)}) collective-permute-start(s32[2,14,3,128]{3,2,1,0:T(4,128)} %get-tuple-element.419), channel_id=1, source_target_pairs={{1,0},{2,1},{3,2},{4,3},{5,4},{6,5},{7,6},{8,7},{9,8},{10,9},{11,1... | collective-permute-start | bytes 129032 | tf_op jit(solution)/shard_map/ppermute | solution.py:21
  45.9 23.6 %collective-permute-start.11 = (s32[2,14,3,128]{3,2,1,0:T(4,128)}, s32[2,14,3,128]{3,2,1,0:T(4,128)}, u32[]{:S(2)}, u32[]{:S(2)}) collective-permute-start(s32[2,14,3,128]{3,2,1,0:T(4,128)} %get-tuple-element.418), channel_id=1, source_target_pairs={{0,1},{1,2},{2,3},{3,4},{4,5},{5,6},{6,7},{7,8},{8,9},{9,10},{10,1... | collective-permute-start | bytes 129032 | tf_op jit(solution)/shard_map/ppermute | solution.py:18
  58.1 7.7 %copy-start = (f32[3,14,3,128]{2,1,0,3:T(8,128)S(1)}, f32[3,14,3,128]{2,1,0,3:T(8,128)}, u32[]{:S(2)}) copy-start(f32[3,14,3,128]{2,1,0,3:T(8,128)} %get-tuple-element.414) | copy-start | bytes 193540
  61.3 9.2 %collective-permute-start.4 = (f32[3,14,3,128]{3,1,2,0:T(8,128)}, f32[3,14,3,128]{3,1,2,0:T(8,128)}, u32[]{:S(2)}, u32[]{:S(2)}) collective-permute-start(f32[3,14,3,128]{3,1,2,0:T(8,128)} %copy.49), channel_id=1, source_target_pairs={{1,0},{2,1},{3,2},{4,3},{5,4},{6,5},{7,6},{8,7},{9,8},{10,9},{11,1... | collective-permute-start | bytes 193544 | tf_op jit(solution)/shard_map/ppermute | solution.py:21
  67.6 6.8 %collective-permute-start.3 = (f32[3,14,3,128]{3,1,2,0:T(8,128)}, f32[3,14,3,128]{3,1,2,0:T(8,128)S(1)}, u32[]{:S(2)}, u32[]{:S(2)}) collective-permute-start(f32[3,14,3,128]{3,1,2,0:T(8,128)} %copy.48), channel_id=1, source_target_pairs={{0,1},{1,2},{2,3},{3,4},{4,5},{5,6},{6,7},{7,8},{8,9},{9,10},{10,1... | collective-permute-start | bytes 193544 | tf_op jit(solution)/shard_map/ppermute | solution.py:18
  90.8 3.2 %copy-start.8 = (f32[24,24]{1,0:T(8,128)S(1)}, f32[24,24]{1,0:T(8,128)}, u32[]{:S(2)}) copy-start(f32[24,24]{1,0:T(8,128)} %constant.279.clone.2) | copy-start | bytes 6916 | tf_op jit(solution)/shard_map/cond
  99.5 8.9 %copy-start.7 = (pred[8,16,3]{1,0,2:T(8,128)(4,1)S(1)}, pred[8,16,3]{1,0,2:T(8,128)(4,1)}, u32[]{:S(2)}) copy-start(pred[8,16,3]{1,0,2:T(8,128)(4,1)} %copy-done.6) | copy-start | bytes 1156
  99.5 9.6 %copy-start.1 = (f32[1,3,8,16,128]{3,2,1,4,0:T(8,128)S(1)}, f32[1,3,8,16,128]{3,2,1,4,0:T(8,128)}, u32[]{:S(2)}) copy-start(f32[1,3,8,16,128]{3,2,1,4,0:T(8,128)} %copy.43) | copy-start | bytes 589828
  99.5 9.6 %copy-start.9 = (pred[128]{0:T(512)(128)(4,1)S(1)}, pred[128]{0:T(512)(128)(4,1)}, u32[]{:S(2)}) copy-start(pred[128]{0:T(512)(128)(4,1)} %get-tuple-element.432) | copy-start | bytes 388
  100.7 7.7 %collective-permute-start.13 = (f32[3,8,16,3]{2,1,0,3:T(8,128)}, f32[3,8,16,3]{2,1,0,3:T(8,128)}, u32[]{:S(2)}, u32[]{:S(2)}) collective-permute-start(f32[3,8,16,3]{2,1,0,3:T(8,128)} %slice.2962), channel_id=1, source_target_pairs={{0,128},{1,129},{2,130},{3,131},{4,132},{5,133},{6,134},{7,135},{8... | collective-permute-start | bytes 13832 | tf_op jit(solution)/shard_map/ppermute | solution.py:29
  113.9 2.6 %copy-start.2 = (f32[1,3,8,16,128]{3,2,1,4,0:T(8,128)S(1)}, f32[1,3,8,16,128]{3,2,1,4,0:T(8,128)}, u32[]{:S(2)}) copy-start(f32[1,3,8,16,128]{3,2,1,4,0:T(8,128)} %get-tuple-element.412) | copy-start | bytes 589828
where the time goes:
time: 119 us; the launch traced here: 118 us
  local copies, waits for them, and re-layouts  50.8 us (43%)
  starting transfers between devices  40.4 us (34%)
  other arithmetic  14.4 us (12%)
  waiting for transfers between devices  7.74 us (7%)
  matrix products  2.9 us (2%)
    ppermute x6, starting transfers between devices, with_halo(): lax.ppermute(lax.slice_in_dim(block, block.shape[dim] - width, None, axis...  19.6 us
    ppermute x6, starting transfers between devices, with_halo(): lax.ppermute(lax.slice_in_dim(block, 0, width, axis=dim), axis, backward)  17.3 us
    cond x25, local copies, waits for them, and re-layouts  16 us
    slice x6, local copies, waits for them, and re-layouts, with_halo(): lax.slice_in_dim(block, block.shape[dim] - width, None, axis=dim)  9.33 us
    unnamed x24, local copies, waits for them, and re-layouts  7.77 us
    slice x3, local copies, waits for them, and re-layouts, with_halo(): lax.slice_in_dim(block, 0, width, axis=dim)  4.85 us
    ppermute x2, waiting for transfers between devices, passed_along(): return lax.ppermute(block, axis, route)  4.72 us
    broadcast_in_dim x1, other arithmetic, per_device(): return (current[None], velocity_now[None])  4.66 us
  transfers between devices with their start and end apart: 14, of which 2 were waited for; matrix products, arithmetic and copies ran while one was open for 27% of the time, Pallas kernels for 0%

commit v1 on v0

v1 whole, which is shorter than its diff:
```python
import math

import jax
import jax.numpy as jnp
import numpy as np
from jax import lax
from jax.experimental import pallas as pl
from jax.experimental.pallas import tpu as pltpu
from jax.sharding import PartitionSpec as P

time_step = 0.1
bond_scale = 1.0
rim = 3
low = 8
MESH = pl.DeviceIdType.MESH
directions = [(1, 0), (-1, 0), (0, 1), (0, -1), (1, 1), (1, -1), (-1, 1), (-1, -1)]
shifts = [1, -1, 2, -2]


def half_offsets():
    table = []
    for delta_x in range(-3, 4):
        for delta_y in range(-3, 4):
            for delta_z in range(-3, 4):
                radius = delta_x * delta_x + delta_y * delta_y + delta_z * delta_z
                if 0 < radius <= 9 and (delta_x, delta_y, delta_z) > (0, 0, 0):
                    table.append((delta_x, delta_y, delta_z))
    return table


def hex_stiffness():
    poisson = 0.3
    lame_first = poisson / ((1.0 + poisson) * (1.0 - 2.0 * poisson))
    shear_modulus = 0.5 / (1.0 + poisson)
    elastic = np.zeros((6, 6))
    elastic[:3, :3] = lame_first
    for axis_id in range(3):
        elastic[axis_id, axis_id] += 2.0 * shear_modulus
        elastic[3 + axis_id, 3 + axis_id] = shear_modulus
    points = [0.5 - 0.5 / math.sqrt(3.0), 0.5 + 0.5 / math.sqrt(3.0)]
    result = np.zeros((24, 24))
    shear_pairs = ((0, 1), (1, 2), (0, 2))
    for along_x in points:
        for along_y in points:
            for along_z in points:
                coords = (along_x, along_y, along_z)
                gradients = np.zeros((3, 8))
                for corner in range(8):
                    corner_bits = (corner >> 2 & 1, corner >> 1 & 1, corner & 1)
                    factors = [
                        coords[axis_id] if corner_bits[axis_id] else 1.0 - coords[axis_id]
                        for axis_id in range(3)
                    ]
                    slopes = [1.0 if corner_bits[axis_id] else -1.0 for axis_id in range(3)]
                    gradients[0, corner] = slopes[0] * factors[1] * factors[2]
                    gradients[1, corner] = factors[0] * slopes[1] * factors[2]
                    gradients[2, corner] = factors[0] * factors[1] * slopes[2]
                strain = np.zeros((6, 24))
                for axis_id in range(3):
                    strain[axis_id, axis_id * 8 : axis_id * 8 + 8] = gradients[axis_id]
                for shear_row, pair in enumerate(shear_pairs):
                    left_axis, right_axis = pair
                    strain[3 + shear_row, left_axis * 8 : left_axis * 8 + 8] = gradients[right_axis]
                    strain[3 + shear_row, right_axis * 8 : right_axis * 8 + 8] = gradients[
                        left_axis
                    ]
                result += strain.T @ elastic @ strain / 8.0
    return result


def modal_stiffness():
    one = np.array([[1.0, -1.0], [1.0, 1.0]])
    corners = np.kron(np.kron(one, one), one)
    basis = np.kron(np.eye(3), corners)
    modal = basis.T @ hex_stiffness() @ basis / 64.0
    modal[np.abs(modal) < 1e-12] = 0.0
    return modal


offsets = half_offsets()
numbers = {offset: number for number, offset in enumerate(offsets)}


def scaled(coefficient, value):
    return value if coefficient == 1 else coefficient * value


def combine(terms):
    total = None
    negative = None
    for coefficient, value in terms:
        if coefficient == 0:
            continue
        if coefficient < 0 and total is None:
            negative = scaled(-coefficient, value) if negative is None else (
                negative + scaled(-coefficient, value)
            )
        elif total is None:
            total = scaled(coefficient, value)
            if negative is not None:
                total = total - negative
                negative = None
        elif coefficient > 0:
            total = total + scaled(coefficient, value)
        else:
            total = total - scaled(-coefficient, value)
    if negative is not None:
        total = -negative
    return total


def turn(value, by):
    return pltpu.roll(value, (-by) % 128, value.ndim - 1)


def kernel(
    disp, vel, mod, words, cmap,
    out_u, out_v,
    B, W, V, CM,
    YS, YSW, YR, YRW, CS, CSW, CR, CRW,
    PS, PX, PY, RS, RR,
    R, R3, WR, WR3, SL, SH,
    load_sem, fs, fr, ws, wr, ps, pr, link_s, link_r,
):
    group = lax.axis_index("group")
    gx = lax.axis_index("gx")
    gy = lax.axis_index("gy")
    size_x = lax.axis_size("gx")
    size_y = lax.axis_size("gy")
    is_zone = group == 0
    is_slab = group == 1
    rows_x, rows_y, depth = V.shape[1], V.shape[2], V.shape[3]
    own_x = slice(rim, rim + rows_x)
    own_y = slice(low, low + rows_y)

    def at(step_x, step_y):
        return (group, gx + step_x, gy + step_y)

    def both(first, second):
        if first is None:
            return second
        return first if second is None else jnp.logical_and(first, second)

    def exists(step_x, step_y):
        test = None
        if step_x:
            test = gx + step_x < size_x if step_x > 0 else gx > 0
        if step_y:
            test = both(test, gy + step_y < size_y if step_y > 0 else gy > 0)
        return test

    loads = [
        pltpu.make_async_copy(disp.at[0], B.at[0:3, own_x, own_y, :], load_sem.at[0]),
        pltpu.make_async_copy(mod.at[0], B.at[3, own_x, own_y, :], load_sem.at[1]),
        pltpu.make_async_copy(words, W.at[:, own_x, own_y, :], load_sem.at[2]),
        pltpu.make_async_copy(cmap, CM, load_sem.at[3]),
        pltpu.make_async_copy(vel.at[0], V, load_sem.at[4]),
    ]
    for load in loads:
        load.start()

    barrier = pltpu.get_barrier_semaphore()
    pl.semaphore_signal(barrier, inc=1, device_id=(1 - group, gx, gy), device_id_type=MESH)
    expected = jnp.int32(1)
    for step_x, step_y in directions:
        present = exists(step_x, step_y)
        expected = expected + present.astype(jnp.int32)

        @pl.when(present)
        def _():
            pl.semaphore_signal(
                barrier, inc=1, device_id=at(step_x, step_y), device_id_type=MESH
            )

    def clear(ref):
        ref[...] = jnp.zeros(ref.shape, ref.dtype)

    @pl.when(gx == 0)
    def _():
        clear(B.at[:, 0:rim])
        clear(W.at[:, 0:rim])
        clear(PX.at[0])
        for side in range(2):
            clear(PY.at[side, 0])

    @pl.when(gx == size_x - 1)
    def _():
        clear(B.at[:, rim + rows_x :])
        clear(PX.at[2])
        for side in range(2):
            clear(PY.at[side, 2])

    for side, edge in ((0, gy == 0), (1, gy == size_y - 1)):

        @pl.when(edge)
        def _():
            clear(YR.at[side])
            clear(YRW.at[side])
            for index in range(3):
                clear(PY.at[side, index])

    for index, (step_x, step_y) in enumerate(directions[4:]):

        @pl.when(jnp.logical_not(exists(-step_x, -step_y)))
        def _():
            clear(CR.at[index])
            if step_x > 0:
                clear(CRW.at[index])

    for load in loads[:3]:
        load.wait()

    def rows_for(step_y):
        return slice(low + rows_y - rim, low + rows_y) if step_y > 0 else slice(low, low + rim)

    for step_y in (1, -1):
        side = 0 if step_y > 0 else 1
        for x in range(rows_x):
            for field in range(4):
                YS[side, field, rim * x : rim * x + rim, :] = B[
                    field, rim + x, rows_for(step_y), :
                ]

        @pl.when(is_zone)
        def _():
            for x in range(rows_x):
                for word in range(2):
                    YSW[side, word, rim * x : rim * x + rim, :] = W[
                        word, rim + x, rows_for(step_y), :
                    ]

    for index, (step_x, step_y) in enumerate(directions[4:]):
        for count in range(2):
            x = rim + (rows_x - 2 + count if step_x > 0 else count)
            for field in range(4):
                CS[index, field, rim * count : rim * count + rim, :] = B[
                    field, x, rows_for(step_y), :
                ]
        if step_x > 0:

            @pl.when(is_zone)
            def _():
                for count in range(2):
                    x = rim + rows_x - 2 + count
                    for word in range(2):
                        CSW[index, word, rim * count : rim * count + rim, :] = W[
                            word, x, rows_for(step_y), :
                        ]

    lanes = lax.broadcasted_iota(jnp.int32, (8, depth), 1)
    wide_lanes = lax.broadcasted_iota(jnp.int32, (rows_y, depth), 1)
    wide_layer = lax.rem(wide_lanes, 3)
    loads[3].wait()

    def packed_map():
        source = lax.broadcasted_iota(jnp.int32, (3 * rows_x, depth), 0)
        target = lax.broadcasted_iota(jnp.int32, (3 * rows_x, depth), 1)
        chosen = jnp.logical_and(
            lax.div(source, rows_x) == lax.rem(target, 3),
            lax.rem(source, rows_x) == lax.rem(lax.div(target, 3), rows_x),
        )
        values = CM[...].reshape(3 * rows_x, rows_y).astype(jnp.float32)
        spread = lax.dot_general(
            values,
            chosen.astype(jnp.float32),
            (((0,), (0,)), ((), ())),
            preferred_element_type=jnp.float32,
        )
        return (spread + 0.5).astype(jnp.int32)

    @pl.when(is_slab)
    def _():
        for tile in range(2):
            rows = slice(low + 8 * tile, low + 8 * tile + 8)
            top = jnp.zeros((8, depth), jnp.float32)
            for c in range(3):
                for x in range(rows_x):
                    place = 3 * (rows_x * c + x)
                    moved = turn(B[c, rim + x, rows, :], depth - 3 - place)
                    top = jnp.where(
                        jnp.logical_and(lanes >= place, lanes < place + 3), moved, top
                    )
            RS[8 * tile : 8 * tile + 8, :] = top
        top = RS[...]
        away = packed_map() - wide_layer
        coupled = jnp.zeros((rows_y, depth), jnp.float32)
        for by in range(-2, 3):
            coupled = jnp.where(away == by, turn(top, by), coupled)
        PS[...] = coupled

    pl.semaphore_wait(barrier, expected)

    def message(source, target, sends, recvs, index, device):
        return pltpu.make_async_remote_copy(
            src_ref=source, dst_ref=target,
            send_sem=sends.at[index], recv_sem=recvs.at[index],
            device_id=device, device_id_type=MESH,
        )

    def field_parts(index):
        step_x, step_y = directions[index]
        if step_y == 0:
            if step_x > 0:
                return B.at[:, rows_x : rows_x + rim, own_y, :], B.at[:, 0:rim, own_y, :]
            return (
                B.at[:, rim : 2 * rim, own_y, :],
                B.at[:, rim + rows_x : 2 * rim + rows_x, own_y, :],
            )
        if step_x == 0:
            side = 0 if step_y > 0 else 1
            return YS.at[side], YR.at[side]
        return CS.at[index - 4], CR.at[index - 4]

    def word_parts(index):
        step_x, step_y = directions[index]
        if step_y == 0:
            return W.at[:, rows_x : rows_x + rim, own_y, :], W.at[:, 0:rim, own_y, :]
        if step_x == 0:
            side = 0 if step_y > 0 else 1
            return YSW.at[side], YRW.at[side]
        return CSW.at[index - 4], CRW.at[index - 4]

    def coupled_parts(index):
        step_x, step_y = directions[index]
        if step_y == 0:
            return PX.at[1], PX.at[1 - step_x]
        if step_y > 0:
            return PX.at[1, 8:16, :], PY.at[0, 1 - step_x]
        return PX.at[1, 0:8, :], PY.at[1, 1 - step_x]

    def send(parts, sends, recvs, index):
        source, target = parts(index)
        return message(source, target, sends, recvs, index, at(*directions[index]))

    has_words = [index for index, (step_x, _) in enumerate(directions) if step_x >= 0]
    order = [0, 1, 4, 5, 6, 7, 2, 3]

    link_up = message(PS, PX.at[1], link_s, link_r, 0, (1 - group, gx, gy))
    link_down = message(RS, RR, link_s, link_r, 1, (1 - group, gx, gy))

    @pl.when(is_slab)
    def _():
        link_up.start()

    for index in order:

        @pl.when(exists(*directions[index]))
        def _():
            send(field_parts, fs, fr, index).start()

    @pl.when(is_zone)
    def _():
        for index in order:
            if index in has_words:

                @pl.when(exists(*directions[index]))
                def _():
                    send(word_parts, ws, wr, index).start()

        link_up.wait_recv()
        for index in order:

            @pl.when(exists(*directions[index]))
            def _():
                send(coupled_parts, ps, pr, index).start()

    loads[4].wait()

    def arrived(index):
        step_x, step_y = directions[index]
        return exists(-step_x, -step_y)

    for index in range(8):

        @pl.when(arrived(index))
        def _():
            send(field_parts, fs, fr, index).wait_recv()

    for side in range(2):
        rows = slice(low - rim, low) if side == 0 else slice(low + rows_y, low + rows_y + rim)
        for x in range(rows_x):
            for field in range(4):
                B[field, rim + x, rows, :] = YR[side, field, rim * x : rim * x + rim, :]
    for index, (step_x, step_y) in enumerate(directions[4:]):
        rows = slice(low - rim, low) if step_y > 0 else slice(low + rows_y, low + rows_y + rim)
        for count in range(2):
            x = 1 + count if step_x > 0 else rim + rows_x + count
            for field in range(4):
                B[field, x, rows, :] = CR[index, field, rim * count : rim * count + rim, :]

    @pl.when(is_zone)
    def _():
        for index in has_words:

            @pl.when(arrived(index))
            def _():
                send(word_parts, ws, wr, index).wait_recv()

        for side in range(2):
            rows = slice(low - rim, low) if side == 0 else slice(low + rows_y, low + rows_y + rim)
            for x in range(rows_x):
                for word in range(2):
                    W[word, rim + x, rows, :] = YRW[side, word, rim * x : rim * x + rim, :]
        for index, (step_x, step_y) in enumerate(directions[4:]):
            if step_x < 0:
                continue
            rows = slice(low - rim, low) if step_y > 0 else slice(low + rows_y, low + rows_y + rim)
            for count in range(2):
                for word in range(2):
                    W[word, 1 + count, rows, :] = CRW[
                        index, word, rim * count : rim * count + rim, :
                    ]

        tiles = [slice(8 * tile, 8 * tile + 8) for tile in range(4)]

        def turn_words(x, carry):
            for word in range(2):
                for rows in tiles:
                    value = W[word, x, rows, :]
                    for place, by in enumerate(shifts):
                        WR[place, word, x, rows, :] = turn(value, by)
            return carry

        lax.fori_loop(1, rim + rows_x, turn_words, 0)

        def turn_modulus(x, carry):
            for rows in tiles:
                value = B[3, x, rows, :]
                for place, by in enumerate(shifts):
                    R[place, 3, x, rows, :] = turn(value, by)
            return carry

        lax.fori_loop(1, 2 * rim + rows_x - 1, turn_modulus, 0)

        for index in range(8):

            @pl.when(arrived(index))
            def _():
                send(coupled_parts, ps, pr, index).wait_recv()

        def turn_fields(x, carry):
            beside = jnp.where(x < rim, 0, jnp.where(x < rim + rows_x, 1, 2))
            inner = lax.rem(x + rows_x - rim, rows_x)
            for tile, rows in enumerate(tiles):
                if tile == 0:
                    packed = PY[0, beside]
                elif tile == 3:
                    packed = PY[1, beside]
                else:
                    packed = PX[beside, 8 * tile - 8 : 8 * tile, :]
                for c in range(3):
                    place = 3 * (rows_x * c + inner)
                    moved = pltpu.roll(packed, lax.rem(depth - place, depth), 1)
                    value = jnp.where(lanes < 3, moved, B[c, x, rows, :])
                    R[4, c, x, rows, :] = value
                    for spot, by in enumerate(shifts):
                        R[spot, c, x, rows, :] = scaled(by if c == 2 else 1, turn(value, by))
            return carry

        lax.fori_loop(0, 2 * rim + rows_x, turn_fields, 0)

        def turn_far(x, carry):
            for rows in tiles[1:3]:
                where = slice(rows.start - low, rows.stop - low)
                for spot, by in enumerate((3, -3)):
                    R3[spot, 0, x, where, :] = turn(B[3, rim + x, rows, :], by)
                    R3[spot, 1, x, where, :] = by * turn(R[4, 2, rim + x, rows, :], by)
                WR3[x, where, :] = turn(W[0, rim + x, rows, :], -3)
            return carry

        lax.fori_loop(0, rows_x, turn_far, 0)

        classes = sorted({tuple(abs(delta) for delta in offset) for offset in offsets})

        def zone_row(x, carry):
            for tile in range(2):
                here = slice(8 * tile, 8 * tile + 8)

                def load(field, delta):
                    delta_x, delta_y, delta_z = delta
                    if abs(delta_z) == 3:
                        return R3[0 if delta_z > 0 else 1, {3: 0, 2: 1}[field], x, here, :]
                    first = low + 8 * tile + delta_y
                    rows = slice(first, first + 8)
                    if delta_z == 0:
                        source = B.at[3] if field == 3 else R.at[4, field]
                        return source[x + rim + delta_x, rows, :]
                    return R[shifts.index(delta_z), field, x + rim + delta_x, rows, :]

                def load_word(word, delta):
                    delta_x, delta_y, delta_z = delta
                    if delta_z == -3:
                        return WR3[x, here, :]
                    first = low + 8 * tile + delta_y
                    rows = slice(first, first + 8)
                    if delta_z == 0:
                        return W[word, x + rim + delta_x, rows, :]
                    return WR[shifts.index(delta_z), word, x + rim + delta_x, rows, :]

                centre = [load(field, (0, 0, 0)) for field in range(4)]
                centre_words = [load_word(word, (0, 0, 0)) for word in range(2)]
                force = [jnp.zeros((8, depth), jnp.float32) for _ in range(3)]
                for kind in classes:
                    weight = (
                        0.5
                        * bond_scale
                        / float(kind[0] ** 2 + kind[1] ** 2 + kind[2] ** 2) ** 1.5
                    )
                    sums = [None, None, None]
                    signs = [(1, -1) if size else (1,) for size in kind]
                    for sign_x in signs[0]:
                        for sign_y in signs[1]:
                            parts = {}
                            for sign_z in signs[2]:
                                delta = (sign_x * kind[0], sign_y * kind[1], sign_z * kind[2])
                                ahead = delta > (0, 0, 0)
                                number = numbers[
                                    delta if ahead else tuple(-value for value in delta)
                                ]
                                word = number // 31
                                flags = (
                                    centre_words[word] if ahead else load_word(word, delta)
                                )
                                intact = (flags & (1 << number % 31)) != 0
                                there = []
                                for c in range(3):
                                    if delta[c]:
                                        coefficient = delta[c]
                                        if c == 2:
                                            coefficient = 1
                                        there.append((coefficient, load(c, delta)))
                                along = combine(there)
                                base = combine(
                                    [(delta[c], centre[c]) for c in range(3) if delta[c]]
                                )
                                strength = (centre[3] + load(3, delta)) * (along - base)
                                parts[sign_z] = jnp.where(intact, strength, 0.0)
                            if kind[2]:
                                plain = parts[1] + parts[-1]
                                tilted = parts[1] - parts[-1]
                            else:
                                plain = parts[1]
                                tilted = None
                            for c, value in enumerate(
                                (plain if kind[0] else None, plain if kind[1] else None, tilted)
                            ):
                                if value is None:
                                    continue
                                sign = (sign_x, sign_y, 1)[c]
                                if sums[c] is None:
                                    sums[c] = value if sign > 0 else -value
                                elif sign > 0:
                                    sums[c] = sums[c] + value
                                else:
                                    sums[c] = sums[c] - value
                    for c in range(3):
                        if sums[c] is not None:
                            force[c] = force[c] + (weight * kind[c]) * sums[c]
                moving = lanes >= 3
                for c in range(3):
                    old = V[c, x, here, :]
                    speed = jnp.where(moving, old + time_step * force[c], old)
                    out_v[0, c, x, here, :] = speed
                    out_u[0, c, x, here, :] = jnp.where(
                        moving, centre[c] + time_step * speed, centre[c]
                    )
                    place = 3 * (rows_x * c + x)
                    moved = pltpu.roll(force[c], place, 1)
                    RS[here, :] = jnp.where(
                        jnp.logical_and(lanes >= place, lanes < place + 3), moved, RS[here, :]
                    )
            return carry

        RS[...] = jnp.zeros(RS.shape, RS.dtype)
        lax.fori_loop(0, rows_x, zone_row, 0)
        link_down.start()

    @pl.when(is_slab)
    def _():
        modal = modal_stiffness()
        last_x = gx == size_x - 1
        last_y = gy == size_y - 1
        row_ids = lax.broadcasted_iota(jnp.int32, (8, depth), 0)
        for tile in range(3):
            rows = slice(8 * tile, 8 * tile + 8)
            next_rows = slice(8 * tile + 1, 8 * tile + 9)
            solid = lanes < depth - 1
            if tile == 2:
                solid = jnp.logical_and(
                    solid, jnp.logical_or(row_ids < 7, jnp.logical_not(last_y))
                )

            def nodes(x):
                result = []
                for c in range(3):
                    here, there = B[c, x, rows, :], B[c, x, next_rows, :]
                    for value in (here + there, there - here):
                        above = turn(value, 1)
                        result += [value + above, above - value]
                return result

            below = nodes(rim - 1)
            carried = None
            for element in range(rows_x + 1):
                above = nodes(rim + element)
                modes = {}
                for c in range(3):
                    for pair in range(4):
                        first, second = below[4 * c + pair], above[4 * c + pair]
                        if pair:
                            modes[8 * c + pair] = first + second
                        modes[8 * c + 4 + pair] = second - first
                below = above
                inside = solid
                if element == rows_x:
                    inside = jnp.logical_and(inside, jnp.logical_not(last_x))
                stiff = jnp.where(inside, B[3, rim - 1 + element, rows, :], 0.0)
                loads_of = {}
                for i in range(24):
                    total = None
                    for j in range(24):
                        if modal[i, j]:
                            term = float(modal[i, j]) * modes[j]
                            total = term if total is None else total + term
                    if total is not None:
                        loads_of[i] = total * stiff
                lows, highs = [], []
                for c in range(3):
                    for pair in range(4):
                        flat, steep = loads_of.get(8 * c + pair), loads_of[8 * c + 4 + pair]
                        lows.append(-steep if flat is None else flat - steep)
                        highs.append(steep if flat is None else flat + steep)
                if element:
                    for c in range(3):
                        halves = []
                        for pair in range(2):
                            flat = lows[4 * c + 2 * pair] + carried[4 * c + 2 * pair]
                            steep = lows[4 * c + 2 * pair + 1] + carried[4 * c + 2 * pair + 1]
                            halves.append((flat - steep) + turn(flat + steep, -1))
                        SL[c, element - 1, rows, :] = halves[0] - halves[1]
                        SH[c, element - 1, rows, :] = halves[0] + halves[1]
                carried = highs

        def inverse_mass(x, tile):
            spread = jnp.where(jnp.logical_or(lanes == 0, lanes == depth - 1), 2.0, 1.0)
            ends_y = jnp.logical_or(
                jnp.logical_and(gy == 0, row_ids + 8 * tile == 0),
                jnp.logical_and(last_y, row_ids + 8 * tile == rows_y - 1),
            )
            spread = spread * jnp.where(ends_y, 2.0, 1.0)
            if x == 0:
                spread = spread * jnp.where(gx == 0, 2.0, 1.0)
            if x == rows_x - 1:
                spread = spread * jnp.where(last_x, 2.0, 1.0)
            return spread

        for x in range(rows_x):
            for tile in range(2):
                here = slice(8 * tile, 8 * tile + 8)
                factor = time_step * inverse_mass(x, tile)
                for c in range(3):
                    force = (
                        SL[c, x, low + 8 * tile : low + 8 * tile + 8, :]
                        + SH[c, x, low + 8 * tile - 1 : low + 8 * tile + 7, :]
                    )
                    out_v[0, c, x, here, :] = V[c, x, here, :] - factor * force

        mapped = packed_map()
        link_down.wait_recv()
        reaction = RR[...]
        shared = jnp.zeros((rows_y, depth), jnp.float32)
        for by in range(-2, 3):
            source_layer = wide_layer + by
            fits = jnp.logical_and(source_layer >= 0, source_layer < 3)
            chosen = jnp.logical_and(fits, turn(mapped, by) == wide_layer)
            shared = shared + jnp.where(chosen, turn(reaction, by), 0.0)
        unclamped = lanes > 0
        for tile in range(2):
            here = slice(8 * tile, 8 * tile + 8)
            part = shared[here, :]
            for x in range(rows_x):
                factor = jnp.where(lanes >= depth - 3, time_step * inverse_mass(x, tile), 0.0)
                for c in range(3):
                    place = 3 * (rows_x * c + x)
                    moved = turn(part, place + 3 - depth)
                    speed = jnp.where(unclamped, out_v[0, c, x, here, :] + factor * moved, 0.0)
                    out_v[0, c, x, here, :] = speed
                    out_u[0, c, x, here, :] = jnp.where(
                        unclamped,
                        B[c, rim + x, low + 8 * tile : low + 8 * tile + 8, :] + time_step * speed,
                        0.0,
                    )

    for index in range(8):

        @pl.when(exists(*directions[index]))
        def _():
            send(field_parts, fs, fr, index).wait_send()

            @pl.when(is_zone)
            def _():
                if index in has_words:
                    send(word_parts, ws, wr, index).wait_send()
                send(coupled_parts, ps, pr, index).wait_send()

    @pl.when(is_slab)
    def _():
        link_up.wait_send()

    @pl.when(is_zone)
    def _():
        link_down.wait_send()


def per_device(displacement, velocity, modulus, bond_words, coupling_map):
    _, _, rows_x, rows_y, depth = displacement.shape
    f32, i32 = jnp.float32, jnp.int32
    wide_x, wide_y = rows_x + 2 * rim, rows_y + 16
    packed = rim * rows_x
    dma = pltpu.SemaphoreType.DMA
    return pl.pallas_call(
        kernel,
        out_shape=(
            jax.ShapeDtypeStruct(displacement.shape, f32),
            jax.ShapeDtypeStruct(velocity.shape, f32),
        ),
        in_specs=[pl.BlockSpec(memory_space=pl.ANY)] * 5,
        out_specs=(pl.BlockSpec(memory_space=pltpu.VMEM),) * 2,
        scratch_shapes=[
            pltpu.VMEM((4, wide_x, wide_y, depth), f32),
            pltpu.VMEM((2, rim + rows_x, wide_y, depth), i32),
            pltpu.VMEM((3, rows_x, rows_y, depth), f32),
            pltpu.VMEM(coupling_map.shape, i32),
            pltpu.VMEM((2, 4, packed, depth), f32),
            pltpu.VMEM((2, 2, packed, depth), i32),
            pltpu.VMEM((2, 4, packed, depth), f32),
            pltpu.VMEM((2, 2, packed, depth), i32),
            pltpu.VMEM((4, 4, 8, depth), f32),
            pltpu.VMEM((2, 2, 8, depth), i32),
            pltpu.VMEM((4, 4, 8, depth), f32),
            pltpu.VMEM((2, 2, 8, depth), i32),
            pltpu.VMEM((rows_y, depth), f32),
            pltpu.VMEM((3, rows_y, depth), f32),
            pltpu.VMEM((2, 3, 8, depth), f32),
            pltpu.VMEM((rows_y, depth), f32),
            pltpu.VMEM((rows_y, depth), f32),
            pltpu.VMEM((5, 4, wide_x, wide_y, depth), f32),
            pltpu.VMEM((2, 2, rows_x, rows_y, depth), f32),
            pltpu.VMEM((4, 2, rim + rows_x, wide_y, depth), i32),
            pltpu.VMEM((rows_x, rows_y, depth), i32),
            pltpu.VMEM((3, rows_x, rows_y + 8, depth), f32),
            pltpu.VMEM((3, rows_x, rows_y + 8, depth), f32),
            dma((5,)), dma((8,)), dma((8,)), dma((8,)), dma((8,)), dma((8,)), dma((8,)),
            dma((2,)), dma((2,)),
        ],
        compiler_params=pltpu.CompilerParams(
            collective_id=0, has_side_effects=True, vmem_limit_bytes=56 * 1024 * 1024
        ),
    )(displacement, velocity, modulus, bond_words, coupling_map)


def solution(mesh):
    return jax.shard_map(
        per_device,
        mesh=mesh,
        in_specs=(
            P("group", None, "gx", "gy", None),
            P("group", None, "gx", "gy", None),
            P("group", "gx", "gy", None),
            P(None, "gx", "gy", None),
            P(None, "gx", "gy"),
        ),
        out_specs=(P("group", None, "gx", "gy", None), P("group", None, "gx", "gy", None)),
        check_vma=False,
    )
```

time: 119 us -> 27.7 us (0.23)
  the two profiles are of different devices: /device:TPU:118 before, /device:TPU:121 now
where the time goes in v1:
time: 27.7 us; the launch traced here: 27.3 us
  Pallas kernels  24.3 us (88%)
  local copies, waits for them, and re-layouts  2.34 us (8%)
  between operations  0.65 us (2%)
    pallas_call x1, Pallas kernels, per_device(): pl.pallas_call(kernel, out_shape=(jax.ShapeDtypeStruct(displacement.shape...  24.3 us
    unnamed x4, local copies, waits for them, and re-layouts  2.34 us

profile of v1, /device:TPU:121, one launch (start us, length us, event | category | flops | bytes accessed | tf_op | source)
XLA Modules:
  0.0 27.3 jit_solution(5462106177699988608)
XLA Ops:
  0.6 24.3 %shard_map.68 = (f32[1,3,8,16,128]{4,3,2,1,0:T(8,128)}, f32[1,3,8,16,128]{4,3,2,1,0:T(8,128)}) custom-call(f32[1,3,8,16,128]{4,3,2,1,0:T(8,128)} %disp.1, f32[1,3,8,16,128]{4,3,2,1,0:T(8,128)} %vel.1, f32[1,8,16,128]{3,2,1,0:T(8,128)} %mod.1, s32[2,8,16,128]{3,2,1,0:T(8,128)} %words.1, s32[3,8,16]{2,1,0:T(8,128)} %cmap.1), custom_call_target="tpu_custom_call" | custom-call | tf_op jit(solution)/shard_map/pallas_call | solution.py:721
  24.9 0.0 copy-start
  24.9 1.7 %copy.9 = f32[1,3,8,16,128]{4,3,2,1,0:T(8,128)} copy(f32[1,3,8,16,128]{4,3,2,1,0:T(8,128)} %get-tuple-element.4) | data formatting | bytes 393216
  26.6 0.0 copy-done
  26.6 0.7 %copy.10 = f32[1,3,8,16,128]{4,3,2,1,0:T(8,128)} copy(f32[1,3,8,16,128]{4,3,2,1,0:T(8,128)S(1)} %copy-done) | data formatting | bytes 393216
Async XLA Ops:
  24.9 1.7 %copy-start = (f32[1,3,8,16,128]{4,3,2,1,0:T(8,128)S(1)}, f32[1,3,8,16,128]{4,3,2,1,0:T(8,128)}, u32[]{:S(2)}) copy-start(f32[1,3,8,16,128]{4,3,2,1,0:T(8,128)} %get-tuple-element.5) | copy-start | bytes 589828

commit v2 on v1

--- a/solution.py
+++ b/solution.py
@@ -79,6 +79,7 @@
 
 offsets = half_offsets()
 numbers = {offset: number for number, offset in enumerate(offsets)}
+bonds = offsets + [tuple(-delta for delta in offset) for offset in offsets]
 
 
 def scaled(coefficient, value):
@@ -105,7 +106,7 @@
         else:
             total = total - scaled(-coefficient, value)
     if negative is not None:
-        total = -negative
+        total = 0.0 - negative
     return total
 
 
@@ -119,8 +120,8 @@
     B, W, V, CM,
     YS, YSW, YR, YRW, CS, CSW, CR, CRW,
     PS, PX, PY, RS, RR,
-    R, R3, WR, WR3, SL, SH,
-    load_sem, fs, fr, ws, wr, ps, pr, link_s, link_r,
+    R, R3, WR, WR3, K, SL, SH,
+    load_sem, fs, fr, ms, mr, ws, wr, ps, pr, link_s, link_r,
 ):
     group = lax.axis_index("group")
     gx = lax.axis_index("gx")
@@ -164,13 +165,22 @@
     expected = jnp.int32(1)
     for step_x, step_y in directions:
         present = exists(step_x, step_y)
-        expected = expected + present.astype(jnp.int32)
+        expected = expected + jnp.where(is_slab, 2, 1) * present.astype(jnp.int32)
 
         @pl.when(present)
         def _():
             pl.semaphore_signal(
                 barrier, inc=1, device_id=at(step_x, step_y), device_id_type=MESH
             )
+
+            @pl.when(is_zone)
+            def _():
+                pl.semaphore_signal(
+                    barrier,
+                    inc=1,
+                    device_id=(1 - group, gx + step_x, gy + step_y),
+                    device_id_type=MESH,
+                )
 
     def clear(ref):
         ref[...] = jnp.zeros(ref.shape, ref.dtype)
@@ -297,19 +307,22 @@
             device_id=device, device_id_type=MESH,
         )
 
-    def field_parts(index):
+    def field_parts(index, fields=slice(0, 3)):
         step_x, step_y = directions[index]
         if step_y == 0:
             if step_x > 0:
-                return B.at[:, rows_x : rows_x + rim, own_y, :], B.at[:, 0:rim, own_y, :]
+                return B.at[fields, rows_x : rows_x + rim, own_y, :], B.at[fields, 0:rim, own_y, :]
             return (
-                B.at[:, rim : 2 * rim, own_y, :],
-                B.at[:, rim + rows_x : 2 * rim + rows_x, own_y, :],
+                B.at[fields, rim : 2 * rim, own_y, :],
+                B.at[fields, rim + rows_x : 2 * rim + rows_x, own_y, :],
             )
         if step_x == 0:
             side = 0 if step_y > 0 else 1
-            return YS.at[side], YR.at[side]
-        return CS.at[index - 4], CR.at[index - 4]
+            return YS.at[side, fields], YR.at[side, fields]
+        return CS.at[index - 4, fields], CR.at[index - 4, fields]
+
+    def modulus_parts(index):
+        return field_parts(index, 3)
 
     def word_parts(index):
         step_x, step_y = directions[index]
@@ -321,26 +334,49 @@
         return CSW.at[index - 4], CRW.at[index - 4]
 
     def coupled_parts(index):
+        if index == 8:
+            return PS, PX.at[1]
         step_x, step_y = directions[index]
         if step_y == 0:
-            return PX.at[1], PX.at[1 - step_x]
+            return PS, PX.at[1 - step_x]
         if step_y > 0:
-            return PX.at[1, 8:16, :], PY.at[0, 1 - step_x]
-        return PX.at[1, 0:8, :], PY.at[1, 1 - step_x]
+            return PS.at[8:16, :], PY.at[0, 1 - step_x]
+        return PS.at[0:8, :], PY.at[1, 1 - step_x]
 
     def send(parts, sends, recvs, index):
         source, target = parts(index)
         return message(source, target, sends, recvs, index, at(*directions[index]))
 
+    def send_coupled(index):
+        source, target = coupled_parts(index)
+        step_x, step_y = directions[index] if index < 8 else (0, 0)
+        device = (1 - group, gx + step_x, gy + step_y)
+        return message(source, target, ps, pr, index, device)
+
     has_words = [index for index, (step_x, _) in enumerate(directions) if step_x >= 0]
     order = [0, 1, 4, 5, 6, 7, 2, 3]
 
-    link_up = message(PS, PX.at[1], link_s, link_r, 0, (1 - group, gx, gy))
-    link_down = message(RS, RR, link_s, link_r, 1, (1 - group, gx, gy))
+    link_down = message(RS, RR, link_s, link_r, 0, (1 - group, gx, gy))
 
     @pl.when(is_slab)
     def _():
-        link_up.start()
+        send_coupled(8).start()
+        for index in order:
+
+            @pl.when(exists(*directions[index]))
+            def _():
+                send_coupled(index).start()
+
+    for index in order:
+
+        @pl.when(exists(*directions[index]))
+        def _():
+            send(modulus_parts, ms, mr, index).start()
+            if index in has_words:
+
+                @pl.when(is_zone)
+                def _():
+                    send(word_parts, ws, wr, index).start()
 
     for index in order:
 
@@ -348,48 +384,66 @@
         def _():
             send(field_parts, fs, fr, index).start()
 
-    @pl.when(is_zone)
-    def _():
-        for index in order:
-            if index in has_words:
-
-                @pl.when(exists(*directions[index]))
-                def _():
-                    send(word_parts, ws, wr, index).start()
-
-        link_up.wait_recv()
-        for index in order:
-
-            @pl.when(exists(*directions[index]))
-            def _():
-                send(coupled_parts, ps, pr, index).start()
-
     loads[4].wait()
 
     def arrived(index):
         step_x, step_y = directions[index]
         return exists(-step_x, -step_y)
 
-    for index in range(8):
-
-        @pl.when(arrived(index))
-        def _():
-            send(field_parts, fs, fr, index).wait_recv()
-
-    for side in range(2):
-        rows = slice(low - rim, low) if side == 0 else slice(low + rows_y, low + rows_y + rim)
-        for x in range(rows_x):
-            for field in range(4):
-                B[field, rim + x, rows, :] = YR[side, field, rim * x : rim * x + rim, :]
-    for index, (step_x, step_y) in enumerate(directions[4:]):
-        rows = slice(low - rim, low) if step_y > 0 else slice(low + rows_y, low + rows_y + rim)
-        for count in range(2):
-            x = 1 + count if step_x > 0 else rim + rows_x + count
-            for field in range(4):
-                B[field, x, rows, :] = CR[index, field, rim * count : rim * count + rim, :]
+    def receive_fields(parts, recvs, fields):
+        for index in range(8):
+
+            @pl.when(arrived(index))
+            def _():
+                send(parts, fs, recvs, index).wait_recv()
+
+        for side in range(2):
+            rows = slice(low - rim, low) if side == 0 else slice(low + rows_y, low + rows_y + rim)
+            for x in range(rows_x):
+                for field in fields:
+                    B[field, rim + x, rows, :] = YR[side, field, rim * x : rim * x + rim, :]
+        for index, (step_x, step_y) in enumerate(directions[4:]):
+            rows = slice(low - rim, low) if step_y > 0 else slice(low + rows_y, low + rows_y + rim)
+            for count in range(2):
+                x = 1 + count if step_x > 0 else rim + rows_x + count
+                for field in fields:
+                    B[field, x, rows, :] = CR[index, field, rim * count : rim * count + rim, :]
 
     @pl.when(is_zone)
     def _():
+        tiles = [slice(8 * tile, 8 * tile + 8) for tile in range(4)]
+        beside_x = (1, 2, rim + rows_x, rim + rows_x + 1)
+
+        def turn_words(x, chosen):
+            for word in range(2):
+                for rows in chosen:
+                    value = W[word, x, rows, :]
+                    for place, by in enumerate(shifts):
+                        WR[place, word, x, rows, :] = turn(value, by)
+
+        def turn_fields(x, chosen, fields):
+            for field in fields:
+                for rows in chosen:
+                    value = B[field, x, rows, :]
+                    for place, by in enumerate(shifts):
+                        R[place, field, x, rows, :] = scaled(
+                            by if field == 2 else 1, turn(value, by)
+                        )
+
+        def turn_own(x, carry):
+            turn_words(rim + x, tiles[1:3])
+            turn_fields(rim + x, tiles[1:3], range(4))
+            for rows in tiles[1:3]:
+                where = slice(rows.start - low, rows.stop - low)
+                for spot, by in enumerate((3, -3)):
+                    R3[spot, 0, x, where, :] = turn(B[3, rim + x, rows, :], by)
+                    R3[spot, 1, x, where, :] = by * turn(B[2, rim + x, rows, :], by)
+                WR3[x, where, :] = turn(W[0, rim + x, rows, :], -3)
+            return carry
+
+        lax.fori_loop(0, rows_x, turn_own, 0)
+
+        receive_fields(modulus_parts, mr, (3,))
         for index in has_words:
 
             @pl.when(arrived(index))
@@ -411,36 +465,76 @@
                         index, word, rim * count : rim * count + rim, :
                     ]
 
-        tiles = [slice(8 * tile, 8 * tile + 8) for tile in range(4)]
-
-        def turn_words(x, carry):
-            for word in range(2):
-                for rows in tiles:
-                    value = W[word, x, rows, :]
-                    for place, by in enumerate(shifts):
-                        WR[place, word, x, rows, :] = turn(value, by)
+        def turn_beside(x, carry):
+            turn_words(rim + x, (tiles[0], tiles[3]))
+            turn_fields(rim + x, (tiles[0], tiles[3]), (3,))
             return carry
 
-        lax.fori_loop(1, rim + rows_x, turn_words, 0)
-
-        def turn_modulus(x, carry):
-            for rows in tiles:
-                value = B[3, x, rows, :]
-                for place, by in enumerate(shifts):
-                    R[place, 3, x, rows, :] = turn(value, by)
+        lax.fori_loop(0, rows_x, turn_beside, 0)
+        for x in beside_x:
+            turn_fields(x, tiles, (3,))
+            if x < rim:
+                turn_words(x, tiles)
+
+        def factor_row(x, carry):
+            for tile in range(2):
+                here = slice(8 * tile, 8 * tile + 8)
+
+                def there(delta):
+                    first = low + 8 * tile + delta[1]
+                    return x + rim + delta[0], slice(first, first + 8)
+
+                def load_modulus(delta):
+                    if abs(delta[2]) == 3:
+                        return R3[0 if delta[2] > 0 else 1, 0, x, here, :]
+                    at_x, rows = there(delta)
+                    if delta[2] == 0:
+                        return B[3, at_x, rows, :]
+                    return R[shifts.index(delta[2]), 3, at_x, rows, :]
+
+                def load_word(word, delta):
+                    if delta[2] == -3:
+                        return WR3[x, here, :]
+                    at_x, rows = there(delta)
+                    if delta[2] == 0:
+                        return W[word, at_x, rows, :]
+                    return WR[shifts.index(delta[2]), word, at_x, rows, :]
+
+                centre = load_modulus((0, 0, 0))
+                centre_words = [load_word(word, (0, 0, 0)) for word in range(2)]
+                for index, delta in enumerate(bonds):
+                    radius = sum(value * value for value in delta)
+                    weight = 0.5 * bond_scale / float(radius) ** 1.5
+                    ahead = delta > (0, 0, 0)
+                    number = numbers[delta if ahead else tuple(-value for value in delta)]
+                    word = number // 31
+                    flags = centre_words[word] if ahead else load_word(word, delta)
+                    intact = (flags & (1 << number % 31)) != 0
+                    K[index, x, here, :] = jnp.where(
+                        intact, weight * (centre + load_modulus(delta)), 0.0
+                    )
             return carry
 
-        lax.fori_loop(1, 2 * rim + rows_x - 1, turn_modulus, 0)
-
+        lax.fori_loop(0, rows_x, factor_row, 0)
+
+        receive_fields(field_parts, fr, range(3))
+
+        def turn_around(x, carry):
+            turn_fields(rim + x, (tiles[0], tiles[3]), range(3))
+            return carry
+
+        lax.fori_loop(0, rows_x, turn_around, 0)
+        for x in beside_x:
+            turn_fields(x, tiles, range(3))
+
+        send_coupled(8).wait_recv()
         for index in range(8):
 
             @pl.when(arrived(index))
             def _():
-                send(coupled_parts, ps, pr, index).wait_recv()
-
-        def turn_fields(x, carry):
-            beside = jnp.where(x < rim, 0, jnp.where(x < rim + rows_x, 1, 2))
-            inner = lax.rem(x + rows_x - rim, rows_x)
+                send_coupled(index).wait_recv()
+
+        def merge(x, inner, beside, outer):
             for tile, rows in enumerate(tiles):
                 if tile == 0:
                     packed = PY[0, beside]
@@ -450,133 +544,154 @@
                     packed = PX[beside, 8 * tile - 8 : 8 * tile, :]
                 for c in range(3):
                     place = 3 * (rows_x * c + inner)
-                    moved = pltpu.roll(packed, lax.rem(depth - place, depth), 1)
-                    value = jnp.where(lanes < 3, moved, B[c, x, rows, :])
-                    R[4, c, x, rows, :] = value
+
+                    def moved(by):
+                        return pltpu.roll(packed, lax.rem(2 * depth - place - by, depth), 1)
+
+                    R[4, c, x, rows, :] = jnp.where(lanes < 3, moved(0), B[c, x, rows, :])
+                    if outer:
+                        continue
                     for spot, by in enumerate(shifts):
-                        R[spot, c, x, rows, :] = scaled(by if c == 2 else 1, turn(value, by))
+                        inside = lanes < 3 - by
+                        if by < 0:
+                            inside = jnp.logical_and(inside, lanes >= -by)
+                        R[spot, c, x, rows, :] = jnp.where(
+                            inside, scaled(by if c == 2 else 1, moved(by)), R[spot, c, x, rows, :]
+                        )
+                    if c == 2 and beside == 1 and tile in (1, 2):
+                        where = slice(rows.start - low, rows.stop - low)
+                        inside = jnp.logical_and(lanes >= 3, lanes < 6)
+                        R3[1, 1, inner, where, :] = jnp.where(
+                            inside, -3 * moved(-3), R3[1, 1, inner, where, :]
+                        )
+
+        def merge_own(x, carry):
+            merge(rim + x, x, 1, False)
             return carry
 
-        lax.fori_loop(0, 2 * rim + rows_x, turn_fields, 0)
-
-        def turn_far(x, carry):
-            for rows in tiles[1:3]:
-                where = slice(rows.start - low, rows.stop - low)
-                for spot, by in enumerate((3, -3)):
-                    R3[spot, 0, x, where, :] = turn(B[3, rim + x, rows, :], by)
-                    R3[spot, 1, x, where, :] = by * turn(R[4, 2, rim + x, rows, :], by)
-                WR3[x, where, :] = turn(W[0, rim + x, rows, :], -3)
-            return carry
-
-        lax.fori_loop(0, rows_x, turn_far, 0)
-
-        classes = sorted({tuple(abs(delta) for delta in offset) for offset in offsets})
-
-        def zone_row(x, carry):
+        lax.fori_loop(0, rows_x, merge_own, 0)
+        for x in range(rim):
+            merge(x, rows_x - rim + x, 0, x == 0)
+            merge(rim + rows_x + x, x, 2, x == rim - 1)
+
+        group_of = 4
+
+        def zone_rows(step, carry):
+            start = step * group_of
             for tile in range(2):
                 here = slice(8 * tile, 8 * tile + 8)
 
-                def load(field, delta):
-                    delta_x, delta_y, delta_z = delta
+                def load(field, move_x, delta_y, delta_z):
                     if abs(delta_z) == 3:
-                        return R3[0 if delta_z > 0 else 1, {3: 0, 2: 1}[field], x, here, :]
+                        return R3[0 if delta_z > 0 else 1, 1, start + move_x, here, :]
                     first = low + 8 * tile + delta_y
-                    rows = slice(first, first + 8)
-                    if delta_z == 0:
-                        source = B.at[3] if field == 3 else R.at[4, field]
-                        return source[x + rim + delta_x, rows, :]
-                    return R[shifts.index(delta_z), field, x + rim + delta_x, rows, :]
-
-                def load_word(word, delta):
-                    delta_x, delta_y, delta_z = delta
-                    if delta_z == -3:
-                        return WR3[x, here, :]
-                    first = low + 8 * tile + delta_y
-                    rows = slice(first, first + 8)
-                    if delta_z == 0:
-                        return W[word, x + rim + delta_x, rows, :]
-                    return WR[shifts.index(delta_z), word, x + rim + delta_x, rows, :]
-
-                centre = [load(field, (0, 0, 0)) for field in range(4)]
-                centre_words = [load_word(word, (0, 0, 0)) for word in range(2)]
-                force = [jnp.zeros((8, depth), jnp.float32) for _ in range(3)]
-                for kind in classes:
-                    weight = (
-                        0.5
-                        * bond_scale
-                        / float(kind[0] ** 2 + kind[1] ** 2 + kind[2] ** 2) ** 1.5
-                    )
-                    sums = [None, None, None]
-                    signs = [(1, -1) if size else (1,) for size in kind]
-                    for sign_x in signs[0]:
-                        for sign_y in signs[1]:
-                            parts = {}
-                            for sign_z in signs[2]:
-                                delta = (sign_x * kind[0], sign_y * kind[1], sign_z * kind[2])
-                                ahead = delta > (0, 0, 0)
-                                number = numbers[
-                                    delta if ahead else tuple(-value for value in delta)
+                    place = 4 if delta_z == 0 else shifts.index(delta_z)
+                    return R[place, field, start + rim + move_x, slice(first, first + 8), :]
+
+                def added(total, sign, value):
+                    if total is None:
+                        return value if sign > 0 else -value
+                    return total + value if sign > 0 else total - value
+
+                centre = [
+                    [load(c, member, 0, 0) for c in range(3)] for member in range(group_of)
+                ]
+                along_x = [[None] * 4 for _ in range(group_of)]
+                along_z = [[None] * 4 for _ in range(group_of)]
+                along_y = [None] * group_of
+                for delta_y in range(-3, 4):
+                    sheet = [None] * group_of
+                    for delta_z in range(-3, 4):
+                        left = 9 - delta_y * delta_y - delta_z * delta_z
+                        if left < 0:
+                            continue
+                        reach = math.isqrt(left)
+                        base = [
+                            combine([(delta_y, centre[member][1]), (delta_z, centre[member][2])])
+                            for member in range(group_of)
+                        ]
+                        line = [None] * group_of
+                        for move_x in range(-reach, group_of + reach):
+                            members = [
+                                member
+                                for member in range(group_of)
+                                if abs(move_x - member) <= reach
+                                and (move_x - member, delta_y, delta_z) != (0, 0, 0)
+                            ]
+                            if not members:
+                                continue
+                            if any(move_x != member for member in members):
+                                away = load(0, move_x, delta_y, delta_z)
+                            side = combine(
+                                [
+                                    (delta_y, load(1, move_x, delta_y, delta_z) if delta_y else None),
+                                    (
+                                        1 if delta_z else 0,
+                                        load(2, move_x, delta_y, delta_z) if delta_z else None,
+                                    ),
                                 ]
-                                word = number // 31
-                                flags = (
-                                    centre_words[word] if ahead else load_word(word, delta)
+                            )
+                            for member in members:
+                                delta_x = move_x - member
+                                stretch = None
+                                if side is not None:
+                                    stretch = side - base[member]
+                                if delta_x:
+                                    gap = away - centre[member][0]
+                                    if stretch is None:
+                                        stretch = scaled(delta_x, gap)
+                                    elif abs(delta_x) == 1:
+                                        stretch = added(stretch, delta_x, gap)
+                                    else:
+                                        stretch = stretch + delta_x * gap
+                                index = bonds.index((delta_x, delta_y, delta_z))
+                                pull = K[index, start + member, here, :] * stretch
+                                line[member] = added(line[member], 1, pull)
+                                if delta_x:
+                                    along_x[member][abs(delta_x)] = added(
+                                        along_x[member][abs(delta_x)], delta_x, pull
+                                    )
+                        for member in range(group_of):
+                            sheet[member] = added(sheet[member], 1, line[member])
+                            if delta_z:
+                                along_z[member][abs(delta_z)] = added(
+                                    along_z[member][abs(delta_z)], delta_z, line[member]
                                 )
-                                intact = (flags & (1 << number % 31)) != 0
-                                there = []
-                                for c in range(3):
-                                    if delta[c]:
-                                        coefficient = delta[c]
-                                        if c == 2:
-                                            coefficient = 1
-                                        there.append((coefficient, load(c, delta)))
-                                along = combine(there)
-                                base = combine(
-                                    [(delta[c], centre[c]) for c in range(3) if delta[c]]
-                                )
-                                strength = (centre[3] + load(3, delta)) * (along - base)
-                                parts[sign_z] = jnp.where(intact, strength, 0.0)
-                            if kind[2]:
-                                plain = parts[1] + parts[-1]
-                                tilted = parts[1] - parts[-1]
-                            else:
-                                plain = parts[1]
-                                tilted = None
-                            for c, value in enumerate(
-                                (plain if kind[0] else None, plain if kind[1] else None, tilted)
-                            ):
-                                if value is None:
-                                    continue
-                                sign = (sign_x, sign_y, 1)[c]
-                                if sums[c] is None:
-                                    sums[c] = value if sign > 0 else -value
-                                elif sign > 0:
-                                    sums[c] = sums[c] + value
-                                else:
-                                    sums[c] = sums[c] - value
+                    if delta_y:
+                        for member in range(group_of):
+                            term = scaled(abs(delta_y), sheet[member])
+                            along_y[member] = added(along_y[member], delta_y, term)
+
+                moving = lanes >= 3
+                for member in range(group_of):
+                    x = start + member
+                    force = [
+                        combine([(size, along_x[member][size]) for size in (1, 2, 3)]),
+                        along_y[member],
+                        combine([(size, along_z[member][size]) for size in (1, 2, 3)]),
+                    ]
                     for c in range(3):
-                        if sums[c] is not None:
-                            force[c] = force[c] + (weight * kind[c]) * sums[c]
-                moving = lanes >= 3
-                for c in range(3):
-                    old = V[c, x, here, :]
-                    speed = jnp.where(moving, old + time_step * force[c], old)
-                    out_v[0, c, x, here, :] = speed
-                    out_u[0, c, x, here, :] = jnp.where(
-                        moving, centre[c] + time_step * speed, centre[c]
-                    )
-                    place = 3 * (rows_x * c + x)
-                    moved = pltpu.roll(force[c], place, 1)
-                    RS[here, :] = jnp.where(
-                        jnp.logical_and(lanes >= place, lanes < place + 3), moved, RS[here, :]
-                    )
+                        old = V[c, x, here, :]
+                        speed = jnp.where(moving, old + time_step * force[c], old)
+                        out_v[0, c, x, here, :] = speed
+                        out_u[0, c, x, here, :] = jnp.where(
+                            moving, centre[member][c] + time_step * speed, centre[member][c]
+                        )
+                        place = 3 * (rows_x * c + x)
+                        moved = pltpu.roll(force[c], place, 1)
+                        RS[here, :] = jnp.where(
+                            jnp.logical_and(lanes >= place, lanes < place + 3), moved, RS[here, :]
+                        )
             return carry
 
         RS[...] = jnp.zeros(RS.shape, RS.dtype)
-        lax.fori_loop(0, rows_x, zone_row, 0)
+        lax.fori_loop(0, rows_x // group_of, zone_rows, 0)
         link_down.start()
 
     @pl.when(is_slab)
     def _():
+        receive_fields(modulus_parts, mr, (3,))
+        receive_fields(field_parts, fr, range(3))
         modal = modal_stiffness()
         last_x = gx == size_x - 1
         last_y = gy == size_y - 1
@@ -696,16 +811,20 @@
         @pl.when(exists(*directions[index]))
         def _():
             send(field_parts, fs, fr, index).wait_send()
-
-            @pl.when(is_zone)
+            send(modulus_parts, ms, mr, index).wait_send()
+            if index in has_words:
+
+                @pl.when(is_zone)
+                def _():
+                    send(word_parts, ws, wr, index).wait_send()
+
+            @pl.when(is_slab)
             def _():
-                if index in has_words:
-                    send(word_parts, ws, wr, index).wait_send()
-                send(coupled_parts, ps, pr, index).wait_send()
+                send_coupled(index).wait_send()
 
     @pl.when(is_slab)
     def _():
-        link_up.wait_send()
+        send_coupled(8).wait_send()
 
     @pl.when(is_zone)
     def _():
@@ -721,10 +840,10 @@
     return pl.pallas_call(
         kernel,
         out_shape=(
-            jax.ShapeDtypeStruct(displacement.shape, f32),
-            jax.ShapeDtypeStruct(velocity.shape, f32),
+            pltpu.VMEM(displacement.shape, f32),
+            pltpu.VMEM(velocity.shape, f32),
         ),
-        in_specs=[pl.BlockSpec(memory_space=pl.ANY)] * 5,
+        in_specs=[pl.BlockSpec(memory_space=pltpu.HBM)] * 5,
         out_specs=(pl.BlockSpec(memory_space=pltpu.VMEM),) * 2,
         scratch_shapes=[
             pltpu.VMEM((4, wide_x, wide_y, depth), f32),
@@ -748,15 +867,19 @@
             pltpu.VMEM((2, 2, rows_x, rows_y, depth), f32),
             pltpu.VMEM((4, 2, rim + rows_x, wide_y, depth), i32),
             pltpu.VMEM((rows_x, rows_y, depth), i32),
+            pltpu.VMEM((len(bonds), rows_x, rows_y, depth), f32),
             pltpu.VMEM((3, rows_x, rows_y + 8, depth), f32),
             pltpu.VMEM((3, rows_x, rows_y + 8, depth), f32),
             dma((5,)), dma((8,)), dma((8,)), dma((8,)), dma((8,)), dma((8,)), dma((8,)),
-            dma((2,)), dma((2,)),
+            dma((9,)), dma((9,)), dma((1,)), dma((1,)),
         ],
         compiler_params=pltpu.CompilerParams(
-            collective_id=0, has_side_effects=True, vmem_limit_bytes=56 * 1024 * 1024
+            collective_id=0, has_side_effects=True, vmem_limit_bytes=24 * 1024 * 1024
         ),
-    )(displacement, velocity, modulus, bond_words, coupling_map)
+    )(*[
+        pltpu.with_memory_space_constraint(value, pltpu.HBM)
+        for value in (displacement, velocity, modulus, bond_words, coupling_map)
+    ])
 
 
 def solution(mesh):

time: 27.7 us -> 22.3 us (0.81); the launches traced: 27.3 us -> 22.2 us
  Pallas kernels: 24.3 us -> 20.2 us
  local copies, waits for them, and re-layouts: 2.34 us -> 1.36 us
    pallas_call x1, Pallas kernels: 24.3 us -> 20.2 us  [per_device(): pl.pallas_call(kernel, out_shape=(pltpu.VMEM(displacement.shape, f32), pl...]
    unnamed x4 -> x2, local copies, waits for them, and re-layouts: 2.34 us -> 1.36 us
where the time goes in v2:
time: 22.3 us; the launch traced here: 22.2 us
  Pallas kernels  20.2 us (91%)
  local copies, waits for them, and re-layouts  1.36 us (6%)
  between operations  0.64 us (3%)
    pallas_call x1, Pallas kernels, per_device(): pl.pallas_call(kernel, out_shape=(pltpu.VMEM(displacement.shape, f32), pl...  20.2 us
    unnamed x2, local copies, waits for them, and re-layouts  1.36 us

profile of v2, /device:TPU:121, one launch (start us, length us, event | category | flops | bytes accessed | tf_op | source)
XLA Modules:
  0.0 22.2 jit_solution(1172325172223820333)
XLA Ops:
  0.6 20.2 %shard_map.68 = (f32[1,3,8,16,128]{4,3,2,1,0:T(8,128)S(1)}, f32[1,3,8,16,128]{4,3,2,1,0:T(8,128)S(1)}) custom-call(f32[1,3,8,16,128]{4,3,2,1,0:T(8,128)} %disp.1, f32[1,3,8,16,128]{4,3,2,1,0:T(8,128)} %vel.1, f32[1,8,16,128]{3,2,1,0:T(8,128)} %mod.1, s32[2,8,16,128]{3,2,1,0:T(8,128)} %words.1, s32[3,8,16]{2,1,0:T(8,128)} %cmap.1), custom_call_target="tpu_custom_call" | custom-call | tf_op jit(solution)/shard_map/pallas_call | solution.py:840
  20.8 0.7 %copy.9 = f32[1,3,8,16,128]{4,3,2,1,0:T(8,128)} copy(f32[1,3,8,16,128]{4,3,2,1,0:T(8,128)S(1)} %get-tuple-element.2) | data formatting | bytes 393216
  21.5 0.7 %copy.10 = f32[1,3,8,16,128]{4,3,2,1,0:T(8,128)} copy(f32[1,3,8,16,128]{4,3,2,1,0:T(8,128)S(1)} %get-tuple-element.3) | data formatting | bytes 393216

commit v3 on v2

--- a/solution.py
+++ b/solution.py
@@ -79,6 +79,15 @@
 
 offsets = half_offsets()
 numbers = {offset: number for number, offset in enumerate(offsets)}
+sheets_of_bonds = [
+    [
+        (delta_y, delta_z)
+        for delta_y in chosen
+        for delta_z in range(-3, 4)
+        if delta_y * delta_y + delta_z * delta_z <= 9
+    ]
+    for chosen in ((0, 3, -3), (1,), (-1,), (2,), (-2,))
+]
 bonds = offsets + [tuple(-delta for delta in offset) for offset in offsets]
 
 
@@ -119,9 +128,9 @@
     out_u, out_v,
     B, W, V, CM,
     YS, YSW, YR, YRW, CS, CSW, CR, CRW,
-    PS, PX, PY, RS, RR,
-    R, R3, WR, WR3, K, SL, SH,
-    load_sem, fs, fr, ms, mr, ws, wr, ps, pr, link_s, link_r,
+    PS, PT, PE, PX, PN, PY, RS, RR,
+    R, R3, WR, WR3, K, FS, SL, SH,
+    load_sem, fs, fr, ms, mr, ws, wr, cs, cr, ps, pr, link_s, link_r,
 ):
     group = lax.axis_index("group")
     gx = lax.axis_index("gx")
@@ -189,14 +198,14 @@
     def _():
         clear(B.at[:, 0:rim])
         clear(W.at[:, 0:rim])
-        clear(PX.at[0])
+        clear(PN.at[0])
         for side in range(2):
             clear(PY.at[side, 0])
 
     @pl.when(gx == size_x - 1)
     def _():
         clear(B.at[:, rim + rows_x :])
-        clear(PX.at[2])
+        clear(PN.at[1])
         for side in range(2):
             clear(PY.at[side, 2])
 
@@ -239,13 +248,21 @@
                         word, rim + x, rows_for(step_y), :
                     ]
 
+    def corner_rows(step_y):
+        if step_y > 0:
+            return slice(low + rows_y - 2, low + rows_y)
+        return slice(low, low + 2)
+
+    def in_corner(field, count):
+        first = 4 * (field % 2) + 2 * count
+        return field // 2, slice(first, first + 2)
+
     for index, (step_x, step_y) in enumerate(directions[4:]):
         for count in range(2):
             x = rim + (rows_x - 2 + count if step_x > 0 else count)
             for field in range(4):
-                CS[index, field, rim * count : rim * count + rim, :] = B[
-                    field, x, rows_for(step_y), :
-                ]
+                tile, rows = in_corner(field, count)
+                CS[index, tile, rows, :] = B[field, x, corner_rows(step_y), :]
         if step_x > 0:
 
             @pl.when(is_zone)
@@ -253,9 +270,8 @@
                 for count in range(2):
                     x = rim + rows_x - 2 + count
                     for word in range(2):
-                        CSW[index, word, rim * count : rim * count + rim, :] = W[
-                            word, x, rows_for(step_y), :
-                        ]
+                        _, rows = in_corner(word, count)
+                        CSW[index, rows, :] = W[word, x, corner_rows(step_y), :]
 
     lanes = lax.broadcasted_iota(jnp.int32, (8, depth), 1)
     wide_lanes = lax.broadcasted_iota(jnp.int32, (rows_y, depth), 1)
@@ -297,6 +313,13 @@
         for by in range(-2, 3):
             coupled = jnp.where(away == by, turn(top, by), coupled)
         PS[...] = coupled
+        for row in range(rows_y):
+            PT[row] = coupled[row : row + 1, :]
+        for side, first in ((0, rows_x - rim), (1, 0)):
+            kept = lax.rem(lanes, 3 * rows_x)
+            kept = jnp.logical_and(kept >= 3 * first, kept < 3 * (first + rim))
+            kept = jnp.logical_and(kept, lanes < 9 * rows_x)
+            PE[side] = jnp.where(kept, coupled[0:8, :], pltpu.roll(coupled[8:16, :], 64, 1))
 
     pl.semaphore_wait(barrier, expected)
 
@@ -307,82 +330,104 @@
             device_id=device, device_id_type=MESH,
         )
 
-    def field_parts(index, fields=slice(0, 3)):
+    def along_gx(ref, step_x, first, count, lead):
+        source = rows_x + first if step_x > 0 else rim + first
+        target = first if step_x > 0 else rim + rows_x + first
+        return (
+            ref.at[lead, source : source + count, own_y, :],
+            ref.at[lead, target : target + count, own_y, :],
+        )
+
+    def modulus_messages(index):
         step_x, step_y = directions[index]
         if step_y == 0:
-            if step_x > 0:
-                return B.at[fields, rows_x : rows_x + rim, own_y, :], B.at[fields, 0:rim, own_y, :]
-            return (
-                B.at[fields, rim : 2 * rim, own_y, :],
-                B.at[fields, rim + rows_x : 2 * rim + rows_x, own_y, :],
-            )
-        if step_x == 0:
-            side = 0 if step_y > 0 else 1
-            return YS.at[side, fields], YR.at[side, fields]
-        return CS.at[index - 4, fields], CR.at[index - 4, fields]
-
-    def modulus_parts(index):
-        return field_parts(index, 3)
-
-    def word_parts(index):
+            return [(along_gx(B, step_x, 0, rim, 3), ms, mr, index)]
+        side = 0 if step_y > 0 else 1
+        return [((YS.at[side, 3], YR.at[side, 3]), ms, mr, index)]
+
+    def field_messages(index):
         step_x, step_y = directions[index]
         if step_y == 0:
-            return W.at[:, rows_x : rows_x + rim, own_y, :], W.at[:, 0:rim, own_y, :]
-        if step_x == 0:
-            side = 0 if step_y > 0 else 1
-            return YSW.at[side], YRW.at[side]
-        return CSW.at[index - 4], CRW.at[index - 4]
-
-    def coupled_parts(index):
-        if index == 8:
-            return PS, PX.at[1]
+            near, far = (1, 0) if step_x > 0 else (0, rim - 1)
+            return [
+                (along_gx(B, step_x, near, 2, slice(0, 3)), fs, fr, index),
+                (along_gx(B, step_x, far, 1, 0), fs, fr, 4 + index),
+            ]
+        side = 0 if step_y > 0 else 1
+        return [((YS.at[side, 0:3], YR.at[side, 0:3]), fs, fr, index)]
+
+    def word_messages(index):
         step_x, step_y = directions[index]
         if step_y == 0:
-            return PS, PX.at[1 - step_x]
-        if step_y > 0:
-            return PS.at[8:16, :], PY.at[0, 1 - step_x]
-        return PS.at[0:8, :], PY.at[1, 1 - step_x]
-
-    def send(parts, sends, recvs, index):
-        source, target = parts(index)
-        return message(source, target, sends, recvs, index, at(*directions[index]))
-
-    def send_coupled(index):
-        source, target = coupled_parts(index)
+            return [
+                (along_gx(W, step_x, 2, 1, slice(0, 2)), ws, wr, index),
+                (along_gx(W, step_x, 0, 2, 1), ws, wr, 4 + index),
+            ]
+        side = 0 if step_y > 0 else 1
+        return [((YSW.at[side], YRW.at[side]), ws, wr, index)]
+
+    def corner_messages(index):
+        return [((CS.at[index - 4], CR.at[index - 4]), cs, cr, index - 4)]
+
+    def corner_word_messages(index):
+        return [((CSW.at[index - 4], CRW.at[index - 4]), cs, cr, index)]
+
+    def copies(messages, index):
+        return [
+            message(source, target, sends, recvs, spot, at(*directions[index]))
+            for (source, target), sends, recvs, spot in messages(index)
+        ]
+
+    def coupled_copy(index):
         step_x, step_y = directions[index] if index < 8 else (0, 0)
+        if index == 8:
+            source, target = PS, PX
+        elif step_y == 0:
+            side = 0 if step_x > 0 else 1
+            source, target = PE.at[side], PN.at[side]
+        elif step_y > 0:
+            source, target = PT.at[rows_y - rim : rows_y], PY.at[0, 1 - step_x]
+        else:
+            source, target = PT.at[0:rim], PY.at[1, 1 - step_x]
         device = (1 - group, gx + step_x, gy + step_y)
         return message(source, target, ps, pr, index, device)
 
-    has_words = [index for index, (step_x, _) in enumerate(directions) if step_x >= 0]
-    order = [0, 1, 4, 5, 6, 7, 2, 3]
-
     link_down = message(RS, RR, link_s, link_r, 0, (1 - group, gx, gy))
+    straight, corners = (0, 1, 2, 3), (4, 5, 6, 7)
+    plan = [(corner_messages, index, False) for index in corners]
+    plan += [(corner_word_messages, index, True) for index in (4, 5)]
+    plan += [(modulus_messages, index, False) for index in (0, 1)]
+    plan += [(word_messages, 0, True)]
+    plan += [(modulus_messages, index, False) for index in (2, 3)]
+    plan += [(word_messages, index, True) for index in (2, 3)]
+    plan += [(field_messages, index, False) for index in straight]
+
+    def start_plan(zone):
+        for messages, index, zone_only in plan:
+            if zone_only and not zone:
+                continue
+
+            @pl.when(exists(*directions[index]))
+            def _():
+                for copy in copies(messages, index):
+                    copy.start()
 
     @pl.when(is_slab)
     def _():
-        send_coupled(8).start()
-        for index in order:
-
-            @pl.when(exists(*directions[index]))
-            def _():
-                send_coupled(index).start()
-
-    for index in order:
-
-        @pl.when(exists(*directions[index]))
-        def _():
-            send(modulus_parts, ms, mr, index).start()
-            if index in has_words:
-
-                @pl.when(is_zone)
+        for index in (4, 5, 6, 7, 0, 1, 8, 2, 3):
+            if index == 8:
+                coupled_copy(8).start()
+            else:
+
+                @pl.when(exists(*directions[index]))
                 def _():
-                    send(word_parts, ws, wr, index).start()
-
-    for index in order:
-
-        @pl.when(exists(*directions[index]))
-        def _():
-            send(field_parts, fs, fr, index).start()
+                    coupled_copy(index).start()
+
+        start_plan(False)
+
+    @pl.when(is_zone)
+    def _():
+        start_plan(True)
 
     loads[4].wait()
 
@@ -390,32 +435,45 @@
         step_x, step_y = directions[index]
         return exists(-step_x, -step_y)
 
-    def receive_fields(parts, recvs, fields):
-        for index in range(8):
+    def receive(messages, indices):
+        for index in indices:
 
             @pl.when(arrived(index))
             def _():
-                send(parts, fs, recvs, index).wait_recv()
-
+                for copy in copies(messages, index):
+                    copy.wait_recv()
+
+    def unpack_rows(side):
+        return slice(low - rim, low) if side == 0 else slice(low + rows_y, low + rows_y + rim)
+
+    def unpack_sides(fields):
         for side in range(2):
-            rows = slice(low - rim, low) if side == 0 else slice(low + rows_y, low + rows_y + rim)
             for x in range(rows_x):
                 for field in fields:
-                    B[field, rim + x, rows, :] = YR[side, field, rim * x : rim * x + rim, :]
-        for index, (step_x, step_y) in enumerate(directions[4:]):
-            rows = slice(low - rim, low) if step_y > 0 else slice(low + rows_y, low + rows_y + rim)
+                    B[field, rim + x, unpack_rows(side), :] = YR[
+                        side, field, rim * x : rim * x + rim, :
+                    ]
+
+    def unpack_corners(first, last, source, target, fields):
+        for index in range(first, last):
+            step_x, step_y = directions[index]
+            where = slice(low - 2, low) if step_y > 0 else slice(low + rows_y, low + rows_y + 2)
             for count in range(2):
                 x = 1 + count if step_x > 0 else rim + rows_x + count
-                for field in fields:
-                    B[field, x, rows, :] = CR[index, field, rim * count : rim * count + rim, :]
+                for field in range(fields):
+                    tile, rows = in_corner(field, count)
+                    part = source[index - 4, rows, :] if fields == 2 else source[
+                        index - 4, tile, rows, :
+                    ]
+                    target[field, x, where, :] = part
 
     @pl.when(is_zone)
     def _():
         tiles = [slice(8 * tile, 8 * tile + 8) for tile in range(4)]
         beside_x = (1, 2, rim + rows_x, rim + rows_x + 1)
 
-        def turn_words(x, chosen):
-            for word in range(2):
+        def turn_words(x, chosen, words_there=(0, 1)):
+            for word in words_there:
                 for rows in chosen:
                     value = W[word, x, rows, :]
                     for place, by in enumerate(shifts):
@@ -443,26 +501,18 @@
 
         lax.fori_loop(0, rows_x, turn_own, 0)
 
-        receive_fields(modulus_parts, mr, (3,))
-        for index in has_words:
-
-            @pl.when(arrived(index))
-            def _():
-                send(word_parts, ws, wr, index).wait_recv()
-
+        receive(corner_messages, corners)
+        receive(corner_word_messages, (4, 5))
+        unpack_corners(4, 8, CR, B, 4)
+        unpack_corners(4, 6, CRW, W, 2)
+        receive(modulus_messages, straight)
+        receive(word_messages, (0, 2, 3))
+        unpack_sides((3,))
         for side in range(2):
-            rows = slice(low - rim, low) if side == 0 else slice(low + rows_y, low + rows_y + rim)
             for x in range(rows_x):
                 for word in range(2):
-                    W[word, rim + x, rows, :] = YRW[side, word, rim * x : rim * x + rim, :]
-        for index, (step_x, step_y) in enumerate(directions[4:]):
-            if step_x < 0:
-                continue
-            rows = slice(low - rim, low) if step_y > 0 else slice(low + rows_y, low + rows_y + rim)
-            for count in range(2):
-                for word in range(2):
-                    W[word, 1 + count, rows, :] = CRW[
-                        index, word, rim * count : rim * count + rim, :
+                    W[word, rim + x, unpack_rows(side), :] = YRW[
+                        side, word, rim * x : rim * x + rim, :
                     ]
 
         def turn_beside(x, carry):
@@ -474,50 +524,76 @@
         for x in beside_x:
             turn_fields(x, tiles, (3,))
             if x < rim:
-                turn_words(x, tiles)
-
-        def factor_row(x, carry):
-            for tile in range(2):
-                here = slice(8 * tile, 8 * tile + 8)
-
-                def there(delta):
-                    first = low + 8 * tile + delta[1]
-                    return x + rim + delta[0], slice(first, first + 8)
-
-                def load_modulus(delta):
-                    if abs(delta[2]) == 3:
-                        return R3[0 if delta[2] > 0 else 1, 0, x, here, :]
-                    at_x, rows = there(delta)
-                    if delta[2] == 0:
-                        return B[3, at_x, rows, :]
-                    return R[shifts.index(delta[2]), 3, at_x, rows, :]
-
-                def load_word(word, delta):
-                    if delta[2] == -3:
-                        return WR3[x, here, :]
-                    at_x, rows = there(delta)
-                    if delta[2] == 0:
-                        return W[word, at_x, rows, :]
-                    return WR[shifts.index(delta[2]), word, at_x, rows, :]
-
-                centre = load_modulus((0, 0, 0))
-                centre_words = [load_word(word, (0, 0, 0)) for word in range(2)]
-                for index, delta in enumerate(bonds):
-                    radius = sum(value * value for value in delta)
-                    weight = 0.5 * bond_scale / float(radius) ** 1.5
-                    ahead = delta > (0, 0, 0)
-                    number = numbers[delta if ahead else tuple(-value for value in delta)]
-                    word = number // 31
-                    flags = centre_words[word] if ahead else load_word(word, delta)
-                    intact = (flags & (1 << number % 31)) != 0
-                    K[index, x, here, :] = jnp.where(
-                        intact, weight * (centre + load_modulus(delta)), 0.0
-                    )
+                turn_words(x, tiles, (0, 1) if x == rim - 1 else (1,))
+
+        group_of = 4
+        blocks = sheets_of_bonds
+
+        def factor_rows(step, carry):
+            tile = lax.rem(step, 2)
+            start = lax.div(step, 2) * group_of
+            here = pl.ds(pl.multiple_of(8 * tile, 8), 8)
+
+            def load_modulus(move_x, delta_y, delta_z):
+                if abs(delta_z) == 3:
+                    return R3[0 if delta_z > 0 else 1, 0, start + move_x, here, :]
+                rows = pl.ds(low + 8 * tile + delta_y, 8)
+                if delta_z == 0:
+                    return B[3, start + rim + move_x, rows, :]
+                return R[shifts.index(delta_z), 3, start + rim + move_x, rows, :]
+
+            def load_word(word, move_x, delta_y, delta_z):
+                if delta_z == -3:
+                    return WR3[start + move_x, here, :]
+                rows = pl.ds(low + 8 * tile + delta_y, 8)
+                if delta_z == 0:
+                    return W[word, start + rim + move_x, rows, :]
+                return WR[shifts.index(delta_z), word, start + rim + move_x, rows, :]
+
+            def block(lines):
+                centre = [load_modulus(member, 0, 0) for member in range(group_of)]
+                centre_words = [
+                    [load_word(word, member, 0, 0) for word in range(2)]
+                    for member in range(group_of)
+                ]
+                for delta_y, delta_z in lines:
+                    reach = math.isqrt(9 - delta_y * delta_y - delta_z * delta_z)
+                    for move_x in range(-reach, group_of + reach):
+                        modulus_there, words_there = None, {}
+                        for member in range(group_of):
+                            delta = (move_x - member, delta_y, delta_z)
+                            if abs(delta[0]) > reach or delta == (0, 0, 0):
+                                continue
+                            radius = sum(value * value for value in delta)
+                            weight = 0.5 * bond_scale / float(radius) ** 1.5
+                            ahead = delta > (0, 0, 0)
+                            number = numbers[delta if ahead else tuple(-value for value in delta)]
+                            word = number // 31
+                            if modulus_there is None:
+                                modulus_there = load_modulus(move_x, delta_y, delta_z)
+                            if ahead:
+                                flags = centre_words[member][word]
+                            else:
+                                if word not in words_there:
+                                    words_there[word] = load_word(word, move_x, delta_y, delta_z)
+                                flags = words_there[word]
+                            intact = (flags & (1 << number % 31)) != 0
+                            K[bonds.index(delta), start + member, here, :] = jnp.where(
+                                intact, weight * (centre[member] + modulus_there), 0.0
+                            )
+
+            for lines in blocks:
+
+                @pl.when(gx >= 0)
+                def _():
+                    block(lines)
+
             return carry
 
-        lax.fori_loop(0, rows_x, factor_row, 0)
-
-        receive_fields(field_parts, fr, range(3))
+        lax.fori_loop(0, 2 * (rows_x // group_of), factor_rows, 0)
+
+        receive(field_messages, straight)
+        unpack_sides(range(3))
 
         def turn_around(x, carry):
             turn_fields(rim + x, (tiles[0], tiles[3]), range(3))
@@ -527,171 +603,194 @@
         for x in beside_x:
             turn_fields(x, tiles, range(3))
 
-        send_coupled(8).wait_recv()
+        coupled_copy(8).wait_recv()
         for index in range(8):
 
             @pl.when(arrived(index))
             def _():
-                send_coupled(index).wait_recv()
-
-        def merge(x, inner, beside, outer):
+                coupled_copy(index).wait_recv()
+
+        def merge(x):
+            beside = 0 if x < rim else 1 if x < rim + rows_x else 2
+            inner = (x - rim) % rows_x
             for tile, rows in enumerate(tiles):
-                if tile == 0:
-                    packed = PY[0, beside]
-                elif tile == 3:
-                    packed = PY[1, beside]
+                extra = 0
+                if tile in (0, 3):
+                    first = 8 - rim if tile == 0 else 0
+                    rows = slice(rows.start + first, rows.start + first + rim)
+                    side = 0 if tile == 0 else 1
+                    packed = PY[side, beside, :, 0, :]
+                elif beside == 1:
+                    packed = PX[8 * tile - 8 : 8 * tile, :]
                 else:
-                    packed = PX[beside, 8 * tile - 8 : 8 * tile, :]
-                for c in range(3):
-                    place = 3 * (rows_x * c + inner)
+                    packed = PN[0 if beside == 0 else 1]
+                    extra = 64 * (tile - 1)
+                outer = x in (0, 2 * rim + rows_x - 1)
+                if outer and tile in (0, 3):
+                    continue
+                lane = lanes if tile in (1, 2) else lanes[0:rim]
+                for c in range(1 if outer else 3):
+                    place = 3 * (rows_x * c + inner) + extra
 
                     def moved(by):
-                        return pltpu.roll(packed, lax.rem(2 * depth - place - by, depth), 1)
-
-                    R[4, c, x, rows, :] = jnp.where(lanes < 3, moved(0), B[c, x, rows, :])
+                        return turn(packed, place + by)
+
+                    R[4, c, x, rows, :] = jnp.where(lane < 3, moved(0), B[c, x, rows, :])
                     if outer:
                         continue
                     for spot, by in enumerate(shifts):
-                        inside = lanes < 3 - by
+                        inside = lane < 3 - by
                         if by < 0:
-                            inside = jnp.logical_and(inside, lanes >= -by)
+                            inside = jnp.logical_and(inside, lane >= -by)
                         R[spot, c, x, rows, :] = jnp.where(
                             inside, scaled(by if c == 2 else 1, moved(by)), R[spot, c, x, rows, :]
                         )
                     if c == 2 and beside == 1 and tile in (1, 2):
                         where = slice(rows.start - low, rows.stop - low)
-                        inside = jnp.logical_and(lanes >= 3, lanes < 6)
+                        inside = jnp.logical_and(lane >= 3, lane < 6)
                         R3[1, 1, inner, where, :] = jnp.where(
                             inside, -3 * moved(-3), R3[1, 1, inner, where, :]
                         )
 
-        def merge_own(x, carry):
-            merge(rim + x, x, 1, False)
-            return carry
-
-        lax.fori_loop(0, rows_x, merge_own, 0)
-        for x in range(rim):
-            merge(x, rows_x - rim + x, 0, x == 0)
-            merge(rim + rows_x + x, x, 2, x == rim - 1)
-
-        group_of = 4
+        for x in range(2 * rim + rows_x):
+            merge(x)
+
+
+        def added(total, sign, value):
+            if total is None:
+                return value if sign > 0 else -value
+            return total + value if sign > 0 else total - value
 
         def zone_rows(step, carry):
-            start = step * group_of
-            for tile in range(2):
-                here = slice(8 * tile, 8 * tile + 8)
-
-                def load(field, move_x, delta_y, delta_z):
-                    if abs(delta_z) == 3:
-                        return R3[0 if delta_z > 0 else 1, 1, start + move_x, here, :]
-                    first = low + 8 * tile + delta_y
-                    place = 4 if delta_z == 0 else shifts.index(delta_z)
-                    return R[place, field, start + rim + move_x, slice(first, first + 8), :]
-
-                def added(total, sign, value):
-                    if total is None:
-                        return value if sign > 0 else -value
-                    return total + value if sign > 0 else total - value
-
+            tile = lax.rem(step, 2)
+            start = lax.div(step, 2) * group_of
+            here = pl.ds(pl.multiple_of(8 * tile, 8), 8)
+
+            def load(field, move_x, delta_y, delta_z):
+                if abs(delta_z) == 3:
+                    return R3[0 if delta_z > 0 else 1, 1, start + move_x, here, :]
+                first = low + 8 * tile + delta_y
+                place = 4 if delta_z == 0 else shifts.index(delta_z)
+                return R[place, field, start + rim + move_x, pl.ds(first, 8), :]
+
+            def block(number, lines):
                 centre = [
                     [load(c, member, 0, 0) for c in range(3)] for member in range(group_of)
                 ]
                 along_x = [[None] * 4 for _ in range(group_of)]
                 along_z = [[None] * 4 for _ in range(group_of)]
-                along_y = [None] * group_of
-                for delta_y in range(-3, 4):
-                    sheet = [None] * group_of
-                    for delta_z in range(-3, 4):
-                        left = 9 - delta_y * delta_y - delta_z * delta_z
-                        if left < 0:
+                sheets = [{} for _ in range(group_of)]
+                for delta_y, delta_z in lines:
+                    reach = math.isqrt(9 - delta_y * delta_y - delta_z * delta_z)
+                    base = [
+                        combine([(delta_y, centre[member][1]), (delta_z, centre[member][2])])
+                        for member in range(group_of)
+                    ]
+                    line = [None] * group_of
+                    for move_x in range(-reach, group_of + reach):
+                        members = [
+                            member
+                            for member in range(group_of)
+                            if abs(move_x - member) <= reach
+                            and (move_x - member, delta_y, delta_z) != (0, 0, 0)
+                        ]
+                        if not members:
                             continue
-                        reach = math.isqrt(left)
-                        base = [
-                            combine([(delta_y, centre[member][1]), (delta_z, centre[member][2])])
-                            for member in range(group_of)
-                        ]
-                        line = [None] * group_of
-                        for move_x in range(-reach, group_of + reach):
-                            members = [
-                                member
-                                for member in range(group_of)
-                                if abs(move_x - member) <= reach
-                                and (move_x - member, delta_y, delta_z) != (0, 0, 0)
+                        if any(move_x != member for member in members):
+                            away = load(0, move_x, delta_y, delta_z)
+                        side = combine(
+                            [
+                                (delta_y, load(1, move_x, delta_y, delta_z) if delta_y else None),
+                                (
+                                    1 if delta_z else 0,
+                                    load(2, move_x, delta_y, delta_z) if delta_z else None,
+                                ),
                             ]
-                            if not members:
-                                continue
-                            if any(move_x != member for member in members):
-                                away = load(0, move_x, delta_y, delta_z)
-                            side = combine(
-                                [
-                                    (delta_y, load(1, move_x, delta_y, delta_z) if delta_y else None),
-                                    (
-                                        1 if delta_z else 0,
-                                        load(2, move_x, delta_y, delta_z) if delta_z else None,
-                                    ),
-                                ]
+                        )
+                        for member in members:
+                            delta_x = move_x - member
+                            stretch = None
+                            if side is not None:
+                                stretch = side - base[member]
+                            if delta_x:
+                                gap = away - centre[member][0]
+                                if stretch is None:
+                                    stretch = scaled(delta_x, gap)
+                                elif abs(delta_x) == 1:
+                                    stretch = added(stretch, delta_x, gap)
+                                else:
+                                    stretch = stretch + delta_x * gap
+                            index = bonds.index((delta_x, delta_y, delta_z))
+                            pull = K[index, start + member, here, :] * stretch
+                            line[member] = added(line[member], 1, pull)
+                            if delta_x:
+                                along_x[member][abs(delta_x)] = added(
+                                    along_x[member][abs(delta_x)], delta_x, pull
+                                )
+                    for member in range(group_of):
+                        if delta_y:
+                            sheets[member][delta_y] = added(
+                                sheets[member].get(delta_y), 1, line[member]
                             )
-                            for member in members:
-                                delta_x = move_x - member
-                                stretch = None
-                                if side is not None:
-                                    stretch = side - base[member]
-                                if delta_x:
-                                    gap = away - centre[member][0]
-                                    if stretch is None:
-                                        stretch = scaled(delta_x, gap)
-                                    elif abs(delta_x) == 1:
-                                        stretch = added(stretch, delta_x, gap)
-                                    else:
-                                        stretch = stretch + delta_x * gap
-                                index = bonds.index((delta_x, delta_y, delta_z))
-                                pull = K[index, start + member, here, :] * stretch
-                                line[member] = added(line[member], 1, pull)
-                                if delta_x:
-                                    along_x[member][abs(delta_x)] = added(
-                                        along_x[member][abs(delta_x)], delta_x, pull
-                                    )
-                        for member in range(group_of):
-                            sheet[member] = added(sheet[member], 1, line[member])
-                            if delta_z:
-                                along_z[member][abs(delta_z)] = added(
-                                    along_z[member][abs(delta_z)], delta_z, line[member]
-                                )
-                    if delta_y:
-                        for member in range(group_of):
-                            term = scaled(abs(delta_y), sheet[member])
-                            along_y[member] = added(along_y[member], delta_y, term)
-
-                moving = lanes >= 3
+                        if delta_z:
+                            along_z[member][abs(delta_z)] = added(
+                                along_z[member][abs(delta_z)], delta_z, line[member]
+                            )
                 for member in range(group_of):
-                    x = start + member
-                    force = [
-                        combine([(size, along_x[member][size]) for size in (1, 2, 3)]),
-                        along_y[member],
-                        combine([(size, along_z[member][size]) for size in (1, 2, 3)]),
+                    part = [
+                        combine([(size, along_x[member][size]) for size in (1, 2, 3)
+                                 if along_x[member][size] is not None]),
+                        combine(list(sheets[member].items())),
+                        combine([(size, along_z[member][size]) for size in (1, 2, 3)
+                                 if along_z[member][size] is not None]),
                     ]
                     for c in range(3):
-                        old = V[c, x, here, :]
-                        speed = jnp.where(moving, old + time_step * force[c], old)
-                        out_v[0, c, x, here, :] = speed
-                        out_u[0, c, x, here, :] = jnp.where(
-                            moving, centre[member][c] + time_step * speed, centre[member][c]
-                        )
-                        place = 3 * (rows_x * c + x)
-                        moved = pltpu.roll(force[c], place, 1)
-                        RS[here, :] = jnp.where(
-                            jnp.logical_and(lanes >= place, lanes < place + 3), moved, RS[here, :]
-                        )
+                        if part[c] is None:
+                            part[c] = jnp.zeros((8, depth), jnp.float32)
+                        if number:
+                            part[c] = part[c] + FS[c, start + member, here, :]
+                        FS[c, start + member, here, :] = part[c]
+
+            for number, lines in enumerate(blocks):
+
+                @pl.when(gx >= 0)
+                def _():
+                    block(number, lines)
+
             return carry
 
-        RS[...] = jnp.zeros(RS.shape, RS.dtype)
-        lax.fori_loop(0, rows_x // group_of, zone_rows, 0)
+        lax.fori_loop(0, 2 * (rows_x // group_of), zone_rows, 0)
+
+        moving = lanes >= 3
+        for tile in range(2):
+            here = slice(8 * tile, 8 * tile + 8)
+            packed = jnp.zeros((8, depth), jnp.float32)
+            for x in range(rows_x):
+                for c in range(3):
+                    place = 3 * (rows_x * c + x)
+                    moved = pltpu.roll(FS[c, x, here, :], place, 1)
+                    packed = jnp.where(
+                        jnp.logical_and(lanes >= place, lanes < place + 3), moved, packed
+                    )
+            RS[here, :] = packed
         link_down.start()
+        for x in range(rows_x):
+            for tile in range(2):
+                here = slice(8 * tile, 8 * tile + 8)
+                for c in range(3):
+                    old = V[c, x, here, :]
+                    place = R[4, c, rim + x, low + 8 * tile : low + 8 * tile + 8, :]
+                    speed = jnp.where(moving, old + time_step * FS[c, x, here, :], old)
+                    out_v[0, c, x, here, :] = speed
+                    out_u[0, c, x, here, :] = jnp.where(moving, place + time_step * speed, place)
 
     @pl.when(is_slab)
     def _():
-        receive_fields(modulus_parts, mr, (3,))
-        receive_fields(field_parts, fr, range(3))
+        receive(corner_messages, corners)
+        receive(modulus_messages, straight)
+        receive(field_messages, straight)
+        unpack_corners(4, 8, CR, B, 4)
+        unpack_sides(range(4))
         modal = modal_stiffness()
         last_x = gx == size_x - 1
         last_y = gy == size_y - 1
@@ -806,29 +905,42 @@
                         0.0,
                     )
 
-    for index in range(8):
-
-        @pl.when(exists(*directions[index]))
-        def _():
-            send(field_parts, fs, fr, index).wait_send()
-            send(modulus_parts, ms, mr, index).wait_send()
-            if index in has_words:
-
-                @pl.when(is_zone)
-                def _():
-                    send(word_parts, ws, wr, index).wait_send()
-
-            @pl.when(is_slab)
+    def end_plan(zone):
+        for messages, index, zone_only in plan:
+            if zone_only and not zone:
+                continue
+
+            @pl.when(exists(*directions[index]))
             def _():
-                send_coupled(index).wait_send()
+                for copy in copies(messages, index):
+                    copy.wait_send()
 
     @pl.when(is_slab)
     def _():
-        send_coupled(8).wait_send()
+        for index in range(8):
+
+            @pl.when(exists(*directions[index]))
+            def _():
+                coupled_copy(index).wait_send()
+
+        coupled_copy(8).wait_send()
+        end_plan(False)
 
     @pl.when(is_zone)
     def _():
+        end_plan(True)
         link_down.wait_send()
+
+
+def store(first_in, second_in, first_out, second_out, sem):
+    copies = [
+        pltpu.make_async_copy(first_in, first_out, sem.at[0]),
+        pltpu.make_async_copy(second_in, second_out, sem.at[1]),
+    ]
+    for copy in copies:
+        copy.start()
+    for copy in copies:
+        copy.wait()
 
 
 def per_device(displacement, velocity, modulus, bond_words, coupling_map):
@@ -837,7 +949,7 @@
     wide_x, wide_y = rows_x + 2 * rim, rows_y + 16
     packed = rim * rows_x
     dma = pltpu.SemaphoreType.DMA
-    return pl.pallas_call(
+    field, speed = pl.pallas_call(
         kernel,
         out_shape=(
             pltpu.VMEM(displacement.shape, f32),
@@ -854,13 +966,16 @@
             pltpu.VMEM((2, 2, packed, depth), i32),
             pltpu.VMEM((2, 4, packed, depth), f32),
             pltpu.VMEM((2, 2, packed, depth), i32),
-            pltpu.VMEM((4, 4, 8, depth), f32),
-            pltpu.VMEM((2, 2, 8, depth), i32),
-            pltpu.VMEM((4, 4, 8, depth), f32),
-            pltpu.VMEM((2, 2, 8, depth), i32),
+            pltpu.VMEM((4, 2, 8, depth), f32),
+            pltpu.VMEM((2, 8, depth), i32),
+            pltpu.VMEM((4, 2, 8, depth), f32),
+            pltpu.VMEM((2, 8, depth), i32),
             pltpu.VMEM((rows_y, depth), f32),
-            pltpu.VMEM((3, rows_y, depth), f32),
-            pltpu.VMEM((2, 3, 8, depth), f32),
+            pltpu.VMEM((rows_y, 1, depth), f32),
+            pltpu.VMEM((2, 8, depth), f32),
+            pltpu.VMEM((rows_y, depth), f32),
+            pltpu.VMEM((2, 8, depth), f32),
+            pltpu.VMEM((2, 3, rim, 1, depth), f32),
             pltpu.VMEM((rows_y, depth), f32),
             pltpu.VMEM((rows_y, depth), f32),
             pltpu.VMEM((5, 4, wide_x, wide_y, depth), f32),
@@ -868,10 +983,11 @@
             pltpu.VMEM((4, 2, rim + rows_x, wide_y, depth), i32),
             pltpu.VMEM((rows_x, rows_y, depth), i32),
             pltpu.VMEM((len(bonds), rows_x, rows_y, depth), f32),
+            pltpu.VMEM((3, rows_x, rows_y, depth), f32),
             pltpu.VMEM((3, rows_x, rows_y + 8, depth), f32),
             pltpu.VMEM((3, rows_x, rows_y + 8, depth), f32),
-            dma((5,)), dma((8,)), dma((8,)), dma((8,)), dma((8,)), dma((8,)), dma((8,)),
-            dma((9,)), dma((9,)), dma((1,)), dma((1,)),
+            dma((5,)), dma((6,)), dma((6,)), dma((4,)), dma((4,)), dma((6,)), dma((6,)),
+            dma((6,)), dma((6,)), dma((9,)), dma((9,)), dma((1,)), dma((1,)),
         ],
         compiler_params=pltpu.CompilerParams(
             collective_id=0, has_side_effects=True, vmem_limit_bytes=24 * 1024 * 1024
@@ -880,6 +996,16 @@
         pltpu.with_memory_space_constraint(value, pltpu.HBM)
         for value in (displacement, velocity, modulus, bond_words, coupling_map)
     ])
+    return pl.pallas_call(
+        store,
+        out_shape=(
+            jax.ShapeDtypeStruct(displacement.shape, f32),
+            jax.ShapeDtypeStruct(velocity.shape, f32),
+        ),
+        in_specs=[pl.BlockSpec(memory_space=pltpu.VMEM)] * 2,
+        out_specs=(pl.BlockSpec(memory_space=pltpu.HBM),) * 2,
+        scratch_shapes=[dma((2,))],
+    )(*[pltpu.with_memory_space_constraint(value, pltpu.VMEM) for value in (field, speed)])
 
 
 def solution(mesh):

time: 22.3 us -> 19.4 us (0.87)
  Pallas kernels: 20.2 us -> 18.7 us
  local copies, waits for them, and re-layouts: 1.36 us -> 0 us
    pallas_call x1, Pallas kernels: 20.2 us -> 17.9 us  [per_device(): pl.pallas_call(kernel, out_shape=(pltpu.VMEM(displacement.shape, f32), pl...]
    unnamed x2 -> x0, local copies, waits for them, and re-layouts: 1.36 us -> none
    pallas_call x0 -> x1, Pallas kernels: none -> 0.76 us  [per_device(): pl.pallas_call(store, out_shape=(jax.ShapeDtypeStruct(displacement.shape,...]
where the time goes in v3:
time: 19.4 us; the launch traced here: 19.3 us
  Pallas kernels  18.7 us (96%)
  between operations  0.64 us (3%)
    pallas_call x1, Pallas kernels, per_device(): pl.pallas_call(kernel, out_shape=(pltpu.VMEM(displacement.shape, f32), pl...  17.9 us
    pallas_call x1, Pallas kernels, per_device(): pl.pallas_call(store, out_shape=(jax.ShapeDtypeStruct(displacement.shape,...  0.76 us

profile of v3, /device:TPU:121, one launch (start us, length us, event | category | flops | bytes accessed | tf_op | source)
XLA Modules:
  0.0 19.3 jit_solution(10560743989177458475)
XLA Ops:
  0.6 17.9 %shard_map.68 = (f32[1,3,8,16,128]{4,3,2,1,0:T(8,128)S(1)}, f32[1,3,8,16,128]{4,3,2,1,0:T(8,128)S(1)}) custom-call(f32[1,3,8,16,128]{4,3,2,1,0:T(8,128)} %disp.1, f32[1,3,8,16,128]{4,3,2,1,0:T(8,128)} %vel.1, f32[1,8,16,128]{3,2,1,0:T(8,128)} %mod.1, s32[2,8,16,128]{3,2,1,0:T(8,128)} %words.1, s32[3,8,16]{2,1,0:T(8,128)} %cmap.1), custom_call_target="tpu_custom_call" | custom-call | tf_op jit(solution)/shard_map/pallas_call | solution.py:952
  18.5 0.8 %shard_map.69 = (f32[1,3,8,16,128]{4,3,2,1,0:T(8,128)}, f32[1,3,8,16,128]{4,3,2,1,0:T(8,128)}) custom-call(f32[1,3,8,16,128]{4,3,2,1,0:T(8,128)S(1)} %get-tuple-element.4.first_in, f32[1,3,8,16,128]{4,3,2,1,0:T(8,128)S(1)} %get-tuple-element.5.second_in), custom_call_target="tpu_custom_call" | custom-call | tf_op jit(solution)/shard_map/pallas_call | solution.py:999

commit v4 on v3

--- a/solution.py
+++ b/solution.py
@@ -501,43 +501,16 @@
 
         lax.fori_loop(0, rows_x, turn_own, 0)
 
-        receive(corner_messages, corners)
-        receive(corner_word_messages, (4, 5))
-        unpack_corners(4, 8, CR, B, 4)
-        unpack_corners(4, 6, CRW, W, 2)
-        receive(modulus_messages, straight)
-        receive(word_messages, (0, 2, 3))
-        unpack_sides((3,))
-        for side in range(2):
-            for x in range(rows_x):
-                for word in range(2):
-                    W[word, rim + x, unpack_rows(side), :] = YRW[
-                        side, word, rim * x : rim * x + rim, :
-                    ]
-
-        def turn_beside(x, carry):
-            turn_words(rim + x, (tiles[0], tiles[3]))
-            turn_fields(rim + x, (tiles[0], tiles[3]), (3,))
-            return carry
-
-        lax.fori_loop(0, rows_x, turn_beside, 0)
-        for x in beside_x:
-            turn_fields(x, tiles, (3,))
-            if x < rim:
-                turn_words(x, tiles, (0, 1) if x == rim - 1 else (1,))
-
         group_of = 4
         blocks = sheets_of_bonds
 
-        def factor_rows(step, carry):
-            tile = lax.rem(step, 2)
-            start = lax.div(step, 2) * group_of
-            here = pl.ds(pl.multiple_of(8 * tile, 8), 8)
+        def factor_rows(start, tile, part):
+            here = slice(8 * tile, 8 * tile + 8)
 
             def load_modulus(move_x, delta_y, delta_z):
                 if abs(delta_z) == 3:
                     return R3[0 if delta_z > 0 else 1, 0, start + move_x, here, :]
-                rows = pl.ds(low + 8 * tile + delta_y, 8)
+                rows = slice(low + 8 * tile + delta_y, low + 8 * tile + delta_y + 8)
                 if delta_z == 0:
                     return B[3, start + rim + move_x, rows, :]
                 return R[shifts.index(delta_z), 3, start + rim + move_x, rows, :]
@@ -545,7 +518,7 @@
             def load_word(word, move_x, delta_y, delta_z):
                 if delta_z == -3:
                     return WR3[start + move_x, here, :]
-                rows = pl.ds(low + 8 * tile + delta_y, 8)
+                rows = slice(low + 8 * tile + delta_y, low + 8 * tile + delta_y + 8)
                 if delta_z == 0:
                     return W[word, start + rim + move_x, rows, :]
                 return WR[shifts.index(delta_z), word, start + rim + move_x, rows, :]
@@ -563,6 +536,10 @@
                         for member in range(group_of):
                             delta = (move_x - member, delta_y, delta_z)
                             if abs(delta[0]) > reach or delta == (0, 0, 0):
+                                continue
+                            beyond_x = not 0 <= start + move_x < rows_x
+                            beyond_y = delta_y < 0 if tile == 0 else delta_y > 0
+                            if part != (2 if beyond_x else 1 if beyond_y else 0):
                                 continue
                             radius = sum(value * value for value in delta)
                             weight = 0.5 * bond_scale / float(radius) ** 1.5
@@ -588,9 +565,42 @@
                 def _():
                     block(lines)
 
+        def factors(part):
+            for start in range(0, rows_x, group_of):
+                for tile in range(2):
+                    factor_rows(start, tile, part)
+
+        factors(0)
+
+        receive(modulus_messages, (2, 3))
+        receive(word_messages, (2, 3))
+        unpack_sides((3,))
+        for side in range(2):
+            for x in range(rows_x):
+                for word in range(2):
+                    W[word, rim + x, unpack_rows(side), :] = YRW[
+                        side, word, rim * x : rim * x + rim, :
+                    ]
+
+        def turn_beside(x, carry):
+            turn_words(rim + x, (tiles[0], tiles[3]))
+            turn_fields(rim + x, (tiles[0], tiles[3]), (3,))
             return carry
 
-        lax.fori_loop(0, 2 * (rows_x // group_of), factor_rows, 0)
+        lax.fori_loop(0, rows_x, turn_beside, 0)
+        factors(1)
+
+        receive(corner_messages, corners)
+        receive(corner_word_messages, (4, 5))
+        unpack_corners(4, 8, CR, B, 4)
+        unpack_corners(4, 6, CRW, W, 2)
+        receive(modulus_messages, (0, 1))
+        receive(word_messages, (0,))
+        for x in beside_x:
+            turn_fields(x, tiles, (3,))
+            if x < rim:
+                turn_words(x, tiles, (0, 1) if x == rim - 1 else (1,))
+        factors(2)
 
         receive(field_messages, straight)
         unpack_sides(range(3))
@@ -603,17 +613,11 @@
         for x in beside_x:
             turn_fields(x, tiles, range(3))
 
-        coupled_copy(8).wait_recv()
-        for index in range(8):
-
-            @pl.when(arrived(index))
-            def _():
-                coupled_copy(index).wait_recv()
-
-        def merge(x):
+        def merge(x, chosen):
             beside = 0 if x < rim else 1 if x < rim + rows_x else 2
             inner = (x - rim) % rows_x
-            for tile, rows in enumerate(tiles):
+            for tile in chosen:
+                rows = tiles[tile]
                 extra = 0
                 if tile in (0, 3):
                     first = 8 - rim if tile == 0 else 0
@@ -652,8 +656,22 @@
                             inside, -3 * moved(-3), R3[1, 1, inner, where, :]
                         )
 
-        for x in range(2 * rim + rows_x):
-            merge(x)
+        own = range(rim, rim + rows_x)
+        coupled_copy(8).wait_recv()
+        for x in own:
+            merge(x, (1, 2))
+        for indices in ((2, 3), (0, 1, 4, 5, 6, 7)):
+            for index in indices:
+
+                @pl.when(arrived(index))
+                def _():
+                    coupled_copy(index).wait_recv()
+
+            for x in range(2 * rim + rows_x):
+                if indices[0] == 2 and x in own:
+                    merge(x, (0, 3))
+                elif indices[0] == 0 and x not in own:
+                    merge(x, range(4))
 
 
         def added(total, sign, value):

time: 19.4 us -> 18 us (0.928); the launches traced: 19.3 us -> 17.7 us
  Pallas kernels: 18.7 us -> 17.1 us
    pallas_call x1, Pallas kernels: 17.9 us -> 16.3 us  [per_device(): pl.pallas_call(kernel, out_shape=(pltpu.VMEM(displacement.shape, f32), pl...]
where the time goes in v4:
time: 18 us; the launch traced here: 17.7 us
  Pallas kernels  17.1 us (95%)
  between operations  0.64 us (4%)
    pallas_call x1, Pallas kernels, per_device(): pl.pallas_call(kernel, out_shape=(pltpu.VMEM(displacement.shape, f32), pl...  16.3 us
    pallas_call x1, Pallas kernels, per_device(): pl.pallas_call(store, out_shape=(jax.ShapeDtypeStruct(displacement.shape,...  0.76 us

profile of v4, /device:TPU:121, one launch (start us, length us, event | category | flops | bytes accessed | tf_op | source)
XLA Modules:
  0.0 17.7 jit_solution(8537838732410096317)
XLA Ops:
  0.6 16.3 %shard_map.68 = (f32[1,3,8,16,128]{4,3,2,1,0:T(8,128)S(1)}, f32[1,3,8,16,128]{4,3,2,1,0:T(8,128)S(1)}) custom-call(f32[1,3,8,16,128]{4,3,2,1,0:T(8,128)} %disp.1, f32[1,3,8,16,128]{4,3,2,1,0:T(8,128)} %vel.1, f32[1,8,16,128]{3,2,1,0:T(8,128)} %mod.1, s32[2,8,16,128]{3,2,1,0:T(8,128)} %words.1, s32[3,8,16]{2,1,0:T(8,128)} %cmap.1), custom_call_target="tpu_custom_call" | custom-call | tf_op jit(solution)/shard_map/pallas_call | solution.py:970
  16.9 0.8 %shard_map.69 = (f32[1,3,8,16,128]{4,3,2,1,0:T(8,128)}, f32[1,3,8,16,128]{4,3,2,1,0:T(8,128)}) custom-call(f32[1,3,8,16,128]{4,3,2,1,0:T(8,128)S(1)} %get-tuple-element.4.first_in, f32[1,3,8,16,128]{4,3,2,1,0:T(8,128)S(1)} %get-tuple-element.5.second_in), custom_call_target="tpu_custom_call" | custom-call | tf_op jit(solution)/shard_map/pallas_call | solution.py:1017

commit v5 on v3

--- a/solution.py
+++ b/solution.py
@@ -159,6 +159,28 @@
             test = both(test, gy + step_y < size_y if step_y > 0 else gy > 0)
         return test
 
+    barrier = pltpu.get_barrier_semaphore()
+    pl.semaphore_signal(barrier, inc=1, device_id=(1 - group, gx, gy), device_id_type=MESH)
+    expected = jnp.int32(1)
+    for step_x, step_y in directions[::-1]:
+        present = exists(step_x, step_y)
+        expected = expected + jnp.where(is_slab, 2, 1) * present.astype(jnp.int32)
+
+        @pl.when(present)
+        def _():
+            pl.semaphore_signal(
+                barrier, inc=1, device_id=at(step_x, step_y), device_id_type=MESH
+            )
+
+            @pl.when(is_zone)
+            def _():
+                pl.semaphore_signal(
+                    barrier,
+                    inc=1,
+                    device_id=(1 - group, gx + step_x, gy + step_y),
+                    device_id_type=MESH,
+                )
+
     loads = [
         pltpu.make_async_copy(disp.at[0], B.at[0:3, own_x, own_y, :], load_sem.at[0]),
         pltpu.make_async_copy(mod.at[0], B.at[3, own_x, own_y, :], load_sem.at[1]),
@@ -168,28 +190,6 @@
     ]
     for load in loads:
         load.start()
-
-    barrier = pltpu.get_barrier_semaphore()
-    pl.semaphore_signal(barrier, inc=1, device_id=(1 - group, gx, gy), device_id_type=MESH)
-    expected = jnp.int32(1)
-    for step_x, step_y in directions:
-        present = exists(step_x, step_y)
-        expected = expected + jnp.where(is_slab, 2, 1) * present.astype(jnp.int32)
-
-        @pl.when(present)
-        def _():
-            pl.semaphore_signal(
-                barrier, inc=1, device_id=at(step_x, step_y), device_id_type=MESH
-            )
-
-            @pl.when(is_zone)
-            def _():
-                pl.semaphore_signal(
-                    barrier,
-                    inc=1,
-                    device_id=(1 - group, gx + step_x, gy + step_y),
-                    device_id_type=MESH,
-                )
 
     def clear(ref):
         ref[...] = jnp.zeros(ref.shape, ref.dtype)
@@ -321,6 +321,112 @@
             kept = jnp.logical_and(kept, lanes < 9 * rows_x)
             PE[side] = jnp.where(kept, coupled[0:8, :], pltpu.roll(coupled[8:16, :], 64, 1))
 
+    tiles = [slice(8 * tile, 8 * tile + 8) for tile in range(4)]
+    beside_x = (1, 2, rim + rows_x, rim + rows_x + 1)
+
+    def turn_words(x, chosen, words_there=(0, 1)):
+        for word in words_there:
+            for rows in chosen:
+                value = W[word, x, rows, :]
+                for place, by in enumerate(shifts):
+                    WR[place, word, x, rows, :] = turn(value, by)
+
+    def turn_fields(x, chosen, fields):
+        for field in fields:
+            for rows in chosen:
+                value = B[field, x, rows, :]
+                for place, by in enumerate(shifts):
+                    R[place, field, x, rows, :] = scaled(
+                        by if field == 2 else 1, turn(value, by)
+                    )
+
+    def turn_own(x, carry):
+        turn_words(rim + x, tiles[1:3])
+        turn_fields(rim + x, tiles[1:3], range(4))
+        for rows in tiles[1:3]:
+            where = slice(rows.start - low, rows.stop - low)
+            for spot, by in enumerate((3, -3)):
+                R3[spot, 0, x, where, :] = turn(B[3, rim + x, rows, :], by)
+                R3[spot, 1, x, where, :] = by * turn(B[2, rim + x, rows, :], by)
+            WR3[x, where, :] = turn(W[0, rim + x, rows, :], -3)
+        return carry
+
+
+    group_of = 4
+    blocks = sheets_of_bonds
+
+    def factor_rows(start, tile, part):
+        here = slice(8 * tile, 8 * tile + 8)
+
+        def load_modulus(move_x, delta_y, delta_z):
+            if abs(delta_z) == 3:
+                return R3[0 if delta_z > 0 else 1, 0, start + move_x, here, :]
+            rows = slice(low + 8 * tile + delta_y, low + 8 * tile + delta_y + 8)
+            if delta_z == 0:
+                return B[3, start + rim + move_x, rows, :]
+            return R[shifts.index(delta_z), 3, start + rim + move_x, rows, :]
+
+        def load_word(word, move_x, delta_y, delta_z):
+            if delta_z == -3:
+                return WR3[start + move_x, here, :]
+            rows = slice(low + 8 * tile + delta_y, low + 8 * tile + delta_y + 8)
+            if delta_z == 0:
+                return W[word, start + rim + move_x, rows, :]
+            return WR[shifts.index(delta_z), word, start + rim + move_x, rows, :]
+
+        def block(lines):
+            centre = [load_modulus(member, 0, 0) for member in range(group_of)]
+            centre_words = [
+                [load_word(word, member, 0, 0) for word in range(2)]
+                for member in range(group_of)
+            ]
+            for delta_y, delta_z in lines:
+                reach = math.isqrt(9 - delta_y * delta_y - delta_z * delta_z)
+                for move_x in range(-reach, group_of + reach):
+                    modulus_there, words_there = None, {}
+                    for member in range(group_of):
+                        delta = (move_x - member, delta_y, delta_z)
+                        if abs(delta[0]) > reach or delta == (0, 0, 0):
+                            continue
+                        beyond_x = not 0 <= start + move_x < rows_x
+                        beyond_y = delta_y < 0 if tile == 0 else delta_y > 0
+                        if part != (2 if beyond_x else 1 if beyond_y else 0):
+                            continue
+                        radius = sum(value * value for value in delta)
+                        weight = 0.5 * bond_scale / float(radius) ** 1.5
+                        ahead = delta > (0, 0, 0)
+                        number = numbers[delta if ahead else tuple(-value for value in delta)]
+                        word = number // 31
+                        if modulus_there is None:
+                            modulus_there = load_modulus(move_x, delta_y, delta_z)
+                        if ahead:
+                            flags = centre_words[member][word]
+                        else:
+                            if word not in words_there:
+                                words_there[word] = load_word(word, move_x, delta_y, delta_z)
+                            flags = words_there[word]
+                        intact = (flags & (1 << number % 31)) != 0
+                        K[bonds.index(delta), start + member, here, :] = jnp.where(
+                            intact, weight * (centre[member] + modulus_there), 0.0
+                        )
+
+        for lines in blocks:
+
+            @pl.when(gx >= 0)
+            def _():
+                block(lines)
+
+    def factors(part):
+        for start in range(0, rows_x, group_of):
+            for tile in range(2):
+                factor_rows(start, tile, part)
+
+
+    @pl.when(is_zone)
+    def _():
+        lax.fori_loop(0, rows_x, turn_own, 0)
+
+
     pl.semaphore_wait(barrier, expected)
 
     def message(source, target, sends, recvs, index, device):
@@ -469,44 +575,10 @@
 
     @pl.when(is_zone)
     def _():
-        tiles = [slice(8 * tile, 8 * tile + 8) for tile in range(4)]
-        beside_x = (1, 2, rim + rows_x, rim + rows_x + 1)
-
-        def turn_words(x, chosen, words_there=(0, 1)):
-            for word in words_there:
-                for rows in chosen:
-                    value = W[word, x, rows, :]
-                    for place, by in enumerate(shifts):
-                        WR[place, word, x, rows, :] = turn(value, by)
-
-        def turn_fields(x, chosen, fields):
-            for field in fields:
-                for rows in chosen:
-                    value = B[field, x, rows, :]
-                    for place, by in enumerate(shifts):
-                        R[place, field, x, rows, :] = scaled(
-                            by if field == 2 else 1, turn(value, by)
-                        )
-
-        def turn_own(x, carry):
-            turn_words(rim + x, tiles[1:3])
-            turn_fields(rim + x, tiles[1:3], range(4))
-            for rows in tiles[1:3]:
-                where = slice(rows.start - low, rows.stop - low)
-                for spot, by in enumerate((3, -3)):
-                    R3[spot, 0, x, where, :] = turn(B[3, rim + x, rows, :], by)
-                    R3[spot, 1, x, where, :] = by * turn(B[2, rim + x, rows, :], by)
-                WR3[x, where, :] = turn(W[0, rim + x, rows, :], -3)
-            return carry
-
-        lax.fori_loop(0, rows_x, turn_own, 0)
-
-        receive(corner_messages, corners)
-        receive(corner_word_messages, (4, 5))
-        unpack_corners(4, 8, CR, B, 4)
-        unpack_corners(4, 6, CRW, W, 2)
-        receive(modulus_messages, straight)
-        receive(word_messages, (0, 2, 3))
+        factors(0)
+
+        receive(modulus_messages, (2, 3))
+        receive(word_messages, (2, 3))
         unpack_sides((3,))
         for side in range(2):
             for x in range(rows_x):
@@ -521,78 +593,9 @@
             return carry
 
         lax.fori_loop(0, rows_x, turn_beside, 0)
-        for x in beside_x:
-            turn_fields(x, tiles, (3,))
-            if x < rim:
-                turn_words(x, tiles, (0, 1) if x == rim - 1 else (1,))
-
-        group_of = 4
-        blocks = sheets_of_bonds
-
-        def factor_rows(step, carry):
-            tile = lax.rem(step, 2)
-            start = lax.div(step, 2) * group_of
-            here = pl.ds(pl.multiple_of(8 * tile, 8), 8)
-
-            def load_modulus(move_x, delta_y, delta_z):
-                if abs(delta_z) == 3:
-                    return R3[0 if delta_z > 0 else 1, 0, start + move_x, here, :]
-                rows = pl.ds(low + 8 * tile + delta_y, 8)
-                if delta_z == 0:
-                    return B[3, start + rim + move_x, rows, :]
-                return R[shifts.index(delta_z), 3, start + rim + move_x, rows, :]
-
-            def load_word(word, move_x, delta_y, delta_z):
-                if delta_z == -3:
-                    return WR3[start + move_x, here, :]
-                rows = pl.ds(low + 8 * tile + delta_y, 8)
-                if delta_z == 0:
-                    return W[word, start + rim + move_x, rows, :]
-                return WR[shifts.index(delta_z), word, start + rim + move_x, rows, :]
-
-            def block(lines):
-                centre = [load_modulus(member, 0, 0) for member in range(group_of)]
-                centre_words = [
-                    [load_word(word, member, 0, 0) for word in range(2)]
-                    for member in range(group_of)
-                ]
-                for delta_y, delta_z in lines:
-                    reach = math.isqrt(9 - delta_y * delta_y - delta_z * delta_z)
-                    for move_x in range(-reach, group_of + reach):
-                        modulus_there, words_there = None, {}
-                        for member in range(group_of):
-                            delta = (move_x - member, delta_y, delta_z)
-                            if abs(delta[0]) > reach or delta == (0, 0, 0):
-                                continue
-                            radius = sum(value * value for value in delta)
-                            weight = 0.5 * bond_scale / float(radius) ** 1.5
-                            ahead = delta > (0, 0, 0)
-                            number = numbers[delta if ahead else tuple(-value for value in delta)]
-                            word = number // 31
-                            if modulus_there is None:
-                                modulus_there = load_modulus(move_x, delta_y, delta_z)
-                            if ahead:
-                                flags = centre_words[member][word]
-                            else:
-                                if word not in words_there:
-                                    words_there[word] = load_word(word, move_x, delta_y, delta_z)
-                                flags = words_there[word]
-                            intact = (flags & (1 << number % 31)) != 0
-                            K[bonds.index(delta), start + member, here, :] = jnp.where(
-                                intact, weight * (centre[member] + modulus_there), 0.0
-                            )
-
-            for lines in blocks:
-
-                @pl.when(gx >= 0)
-                def _():
-                    block(lines)
-
-            return carry
-
-        lax.fori_loop(0, 2 * (rows_x // group_of), factor_rows, 0)
-
-        receive(field_messages, straight)
+        factors(1)
+
+        receive(field_messages, (2, 3))
         unpack_sides(range(3))
 
         def turn_around(x, carry):
@@ -600,20 +603,12 @@
             return carry
 
         lax.fori_loop(0, rows_x, turn_around, 0)
-        for x in beside_x:
-            turn_fields(x, tiles, range(3))
-
-        coupled_copy(8).wait_recv()
-        for index in range(8):
-
-            @pl.when(arrived(index))
-            def _():
-                coupled_copy(index).wait_recv()
-
-        def merge(x):
+
+        def merge(x, chosen):
             beside = 0 if x < rim else 1 if x < rim + rows_x else 2
             inner = (x - rim) % rows_x
-            for tile, rows in enumerate(tiles):
+            for tile in chosen:
+                rows = tiles[tile]
                 extra = 0
                 if tile in (0, 3):
                     first = 8 - rim if tile == 0 else 0
@@ -652,28 +647,23 @@
                             inside, -3 * moved(-3), R3[1, 1, inner, where, :]
                         )
 
-        for x in range(2 * rim + rows_x):
-            merge(x)
-
 
         def added(total, sign, value):
             if total is None:
                 return value if sign > 0 else -value
             return total + value if sign > 0 else total - value
 
-        def zone_rows(step, carry):
-            tile = lax.rem(step, 2)
-            start = lax.div(step, 2) * group_of
-            here = pl.ds(pl.multiple_of(8 * tile, 8), 8)
+        def zone_rows(start, tile, part):
+            here = slice(8 * tile, 8 * tile + 8)
 
             def load(field, move_x, delta_y, delta_z):
                 if abs(delta_z) == 3:
                     return R3[0 if delta_z > 0 else 1, 1, start + move_x, here, :]
                 first = low + 8 * tile + delta_y
                 place = 4 if delta_z == 0 else shifts.index(delta_z)
-                return R[place, field, start + rim + move_x, pl.ds(first, 8), :]
-
-            def block(number, lines):
+                return R[place, field, start + rim + move_x, slice(first, first + 8), :]
+
+            def block(lines):
                 centre = [
                     [load(c, member, 0, 0) for c in range(3)] for member in range(group_of)
                 ]
@@ -688,6 +678,8 @@
                     ]
                     line = [None] * group_of
                     for move_x in range(-reach, group_of + reach):
+                        if part != (0 if 0 <= start + move_x < rows_x else 1):
+                            continue
                         members = [
                             member
                             for member in range(group_of)
@@ -728,6 +720,8 @@
                                     along_x[member][abs(delta_x)], delta_x, pull
                                 )
                     for member in range(group_of):
+                        if line[member] is None:
+                            continue
                         if delta_y:
                             sheets[member][delta_y] = added(
                                 sheets[member].get(delta_y), 1, line[member]
@@ -737,7 +731,7 @@
                                 along_z[member][abs(delta_z)], delta_z, line[member]
                             )
                 for member in range(group_of):
-                    part = [
+                    sums = [
                         combine([(size, along_x[member][size]) for size in (1, 2, 3)
                                  if along_x[member][size] is not None]),
                         combine(list(sheets[member].items())),
@@ -745,21 +739,57 @@
                                  if along_z[member][size] is not None]),
                     ]
                     for c in range(3):
-                        if part[c] is None:
-                            part[c] = jnp.zeros((8, depth), jnp.float32)
-                        if number:
-                            part[c] = part[c] + FS[c, start + member, here, :]
-                        FS[c, start + member, here, :] = part[c]
-
-            for number, lines in enumerate(blocks):
+                        if sums[c] is not None:
+                            FS[c, start + member, here, :] = FS[c, start + member, here, :] + sums[c]
+
+            for lines in blocks:
 
                 @pl.when(gx >= 0)
                 def _():
-                    block(number, lines)
-
-            return carry
-
-        lax.fori_loop(0, 2 * (rows_x // group_of), zone_rows, 0)
+                    block(lines)
+
+        def forces(part):
+            for start in range(0, rows_x, group_of):
+                for tile in range(2):
+                    zone_rows(start, tile, part)
+
+        def receive_coupled(indices):
+            for index in indices:
+
+                @pl.when(arrived(index))
+                def _():
+                    coupled_copy(index).wait_recv()
+
+        own = range(rim, rim + rows_x)
+        FS[...] = jnp.zeros(FS.shape, FS.dtype)
+        coupled_copy(8).wait_recv()
+        for x in own:
+            merge(x, (1, 2))
+        receive_coupled((2, 3))
+        for x in own:
+            merge(x, (0, 3))
+        forces(0)
+
+        receive(corner_messages, corners)
+        receive(corner_word_messages, (4, 5))
+        unpack_corners(4, 8, CR, B, 4)
+        unpack_corners(4, 6, CRW, W, 2)
+        receive(modulus_messages, (0, 1))
+        receive(word_messages, (0,))
+        for x in beside_x:
+            turn_fields(x, tiles, (3,))
+            if x < rim:
+                turn_words(x, tiles, (0, 1) if x == rim - 1 else (1,))
+        factors(2)
+
+        receive(field_messages, (0, 1))
+        for x in beside_x:
+            turn_fields(x, tiles, range(3))
+        receive_coupled((0, 1, 4, 5, 6, 7))
+        for x in range(2 * rim + rows_x):
+            if x not in own:
+                merge(x, range(4))
+        forces(1)
 
         moving = lanes >= 3
         for tile in range(2):

time: 19.4 us -> 17.7 us (0.912)
  the two profiles are of different devices: /device:TPU:121 before, /device:TPU:125 now
where the time goes in v5:
time: 17.7 us; the launch traced here: 17.6 us
  Pallas kernels  16.9 us (95%)
  between operations  0.64 us (4%)
    pallas_call x1, Pallas kernels, per_device(): pl.pallas_call(kernel, out_shape=(pltpu.VMEM(displacement.shape, f32), pl...  16.2 us
    pallas_call x1, Pallas kernels, per_device(): pl.pallas_call(store, out_shape=(jax.ShapeDtypeStruct(displacement.shape,...  0.76 us

profile of v5, /device:TPU:125, one launch (start us, length us, event | category | flops | bytes accessed | tf_op | source)
XLA Modules:
  0.0 17.6 jit_solution(4075966660647381478)
XLA Ops:
  0.6 16.2 %shard_map.68 = (f32[1,3,8,16,128]{4,3,2,1,0:T(8,128)S(1)}, f32[1,3,8,16,128]{4,3,2,1,0:T(8,128)S(1)}) custom-call(f32[1,3,8,16,128]{4,3,2,1,0:T(8,128)} %disp.1, f32[1,3,8,16,128]{4,3,2,1,0:T(8,128)} %vel.1, f32[1,8,16,128]{3,2,1,0:T(8,128)} %mod.1, s32[2,8,16,128]{3,2,1,0:T(8,128)} %words.1, s32[3,8,16]{2,1,0:T(8,128)} %cmap.1), custom_call_target="tpu_custom_call" | custom-call | tf_op jit(solution)/shard_map/pallas_call | solution.py:982
  16.8 0.8 %shard_map.69 = (f32[1,3,8,16,128]{4,3,2,1,0:T(8,128)}, f32[1,3,8,16,128]{4,3,2,1,0:T(8,128)}) custom-call(f32[1,3,8,16,128]{4,3,2,1,0:T(8,128)S(1)} %get-tuple-element.4.first_in, f32[1,3,8,16,128]{4,3,2,1,0:T(8,128)S(1)} %get-tuple-element.5.second_in), custom_call_target="tpu_custom_call" | custom-call | tf_op jit(solution)/shard_map/pallas_call | solution.py:1029

commit v6 on v5

--- a/solution.py
+++ b/solution.py
@@ -500,13 +500,14 @@
 
     link_down = message(RS, RR, link_s, link_r, 0, (1 - group, gx, gy))
     straight, corners = (0, 1, 2, 3), (4, 5, 6, 7)
-    plan = [(corner_messages, index, False) for index in corners]
+    plan = [(modulus_messages, index, False) for index in (2, 3)]
+    plan += [(word_messages, index, True) for index in (2, 3)]
+    plan += [(field_messages, index, False) for index in (2, 3)]
+    plan += [(corner_messages, index, False) for index in corners]
     plan += [(corner_word_messages, index, True) for index in (4, 5)]
     plan += [(modulus_messages, index, False) for index in (0, 1)]
     plan += [(word_messages, 0, True)]
-    plan += [(modulus_messages, index, False) for index in (2, 3)]
-    plan += [(word_messages, index, True) for index in (2, 3)]
-    plan += [(field_messages, index, False) for index in straight]
+    plan += [(field_messages, index, False) for index in (0, 1)]
 
     def start_plan(zone):
         for messages, index, zone_only in plan:
@@ -520,7 +521,7 @@
 
     @pl.when(is_slab)
     def _():
-        for index in (4, 5, 6, 7, 0, 1, 8, 2, 3):
+        for index in (8, 2, 3, 4, 5, 6, 7, 0, 1):
             if index == 8:
                 coupled_copy(8).start()
             else:

time: 17.7 us -> 17.7 us (level)
  no operation moved by 1% of the time
where the time goes in v6:
time: 17.7 us; the launch traced here: 17.6 us
  Pallas kernels  16.9 us (95%)
  between operations  0.64 us (4%)
    pallas_call x1, Pallas kernels, per_device(): pl.pallas_call(kernel, out_shape=(pltpu.VMEM(displacement.shape, f32), pl...  16.2 us
    pallas_call x1, Pallas kernels, per_device(): pl.pallas_call(store, out_shape=(jax.ShapeDtypeStruct(displacement.shape,...  0.76 us

profile of v6, /device:TPU:125, one launch (start us, length us, event | category | flops | bytes accessed | tf_op | source)
XLA Modules:
  0.0 17.6 jit_solution(9804785057045185807)
XLA Ops:
  0.6 16.2 %shard_map.68 = (f32[1,3,8,16,128]{4,3,2,1,0:T(8,128)S(1)}, f32[1,3,8,16,128]{4,3,2,1,0:T(8,128)S(1)}) custom-call(f32[1,3,8,16,128]{4,3,2,1,0:T(8,128)} %disp.1, f32[1,3,8,16,128]{4,3,2,1,0:T(8,128)} %vel.1, f32[1,8,16,128]{3,2,1,0:T(8,128)} %mod.1, s32[2,8,16,128]{3,2,1,0:T(8,128)} %words.1, s32[3,8,16]{2,1,0:T(8,128)} %cmap.1), custom_call_target="tpu_custom_call" | custom-call | tf_op jit(solution)/shard_map/pallas_call | solution.py:983
  16.8 0.8 %shard_map.69 = (f32[1,3,8,16,128]{4,3,2,1,0:T(8,128)}, f32[1,3,8,16,128]{4,3,2,1,0:T(8,128)}) custom-call(f32[1,3,8,16,128]{4,3,2,1,0:T(8,128)S(1)} %get-tuple-element.4.first_in, f32[1,3,8,16,128]{4,3,2,1,0:T(8,128)S(1)} %get-tuple-element.5.second_in), custom_call_target="tpu_custom_call" | custom-call | tf_op jit(solution)/shard_map/pallas_call | solution.py:1030
